TPU v7x, 256 devices: a whole 4x4x8 slice. The times are simulated.
256 devices in a mesh: role: 4 (over z_lo), dp: 16 (over z_hi, x, core), tp: 4 (over y).
Axes of the slice: x: 4, y: 4, z: 8 (z_hi: 2, z_lo: 4; z = z_hi * 4 + z_lo), core: 2. Of those that a mesh axis runs over, the one named last changes fastest.
Arguments:
- activations: bfloat16 [16384, 8192], P(('role', 'dp'), 'tp'), may hold values from -6 to 6
- cotangent: bfloat16 [16384, 14336], P(('role', 'dp'), 'tp'), may hold values from -6 to 6
- block_keep: int32 [64], P(('role', 'dp')), may hold values 0 or 1
- input_factor: float32 [64, 8192], P(('role', 'dp'), 'tp'), may hold values from -0.5 to 0.5
- input_mean: float32 [64, 8192], P(('role', 'dp'), 'tp'), may hold values from -6 to 6
- input_square: float32 [64, 8192], P(('role', 'dp'), 'tp'), may hold values from 0.5 to 4
- output_factor: float32 [64, 14336], P(('role', 'dp'), 'tp'), may hold values from -0.3125 to 0.3125
- output_mean: float32 [64, 14336], P(('role', 'dp'), 'tp'), may hold values from -6 to 6
- output_square: float32 [64, 14336], P(('role', 'dp'), 'tp'), may hold values from 0.5 to 4
- frozen_base_rows: bfloat16 [14336, 8192], P(('dp', 'tp')), may hold values from -0.0625 to 0.0625
- prompts: bfloat16 [1024, 8192], P(('role', 'dp', 'tp')), may hold values from -6 to 6
Outputs:
- updated_input: float32 [64, 8192], P(('role', 'dp'), 'tp')
- updated_output: float32 [64, 14336], P(('role', 'dp'), 'tp')
- mean_input: float32 [64, 8192], P(('role', 'dp'), 'tp')
- mean_output: float32 [64, 14336], P(('role', 'dp'), 'tp')
- square_input: float32 [64, 8192], P(('role', 'dp'), 'tp')
- square_output: float32 [64, 14336], P(('role', 'dp'), 'tp')
- merged_weight_rows: bfloat16 [14336, 8192], P(('dp', 'tp'))
- projected: bfloat16 [14336, 1024], P(('dp', 'tp'), 'role')
All inputs are finite; a program needn't handle non-finite values. No bound on the sum of `block_keep` on one device may be relied on, other than what follows from the above.
Results may differ from a plain program's by a relative error of at most 0.006.
Values may be sent and summed in bfloat16 or wider, within the bound.
A program may use at most 64 MiB of HBM per device.

v0:
```python
import jax
import jax.numpy as jnp
from jax import lax
from jax.sharding import PartitionSpec as P

ROLLOUT_TOKENS = 256


adapter_scale = 2.0
learn_rate = 0.004
beta_one = 0.9
beta_two = 0.95
epsilon = 1e-08
first_fix = 1.0 - 0.9**20
second_fix = 1.0 - 0.95**20


def sent_together(arrays, axis, dim, along):
    ends, at = ([], 0)
    for a in arrays[:-1]:
        at += a.shape[along]
        ends.append(at)
    both = jnp.concatenate(arrays, axis=along)
    return tuple(jnp.split(lax.all_gather(both, axis, axis=dim, tiled=True), ends, axis=along))


def copy_for_each(shard, axis):
    copies = jnp.broadcast_to(shard, (lax.axis_size(axis), *shard.shape))
    return lax.all_to_all(copies, axis, split_axis=0, concat_axis=0, tiled=True)


def taken_together(shard, axis):
    everything = copy_for_each(shard, axis)
    return jnp.sum(everything, axis=0)


def together(arrays, axis):
    ends = [0]
    for a in arrays:
        ends.append(ends[-1] + a.size)
    running = taken_together(jnp.concatenate([a.ravel() for a in arrays]), axis)
    return tuple((running[b:e].reshape(a.shape) for a, b, e in zip(arrays, ends, ends[1:])))


def in_blocks(shard, dim, peers):
    lengths = shard.shape
    pieces = shard.reshape(*lengths[:dim], peers, lengths[dim] // peers, *lengths[dim + 1 :])
    return jnp.moveaxis(pieces, dim, 0)


def summed_on_arrival(shard, axis, dim):
    peers = lax.axis_size(axis)
    pieces = lax.all_to_all(in_blocks(shard, dim, peers), axis, 0, 0, tiled=True)
    return jnp.sum(pieces, axis=0)


def sent_together_2(arrays, axis, dim, along):
    both = jnp.concatenate(arrays, axis=along)
    whole, at, finished = (summed_on_arrival(both, axis, dim), 0, [])
    for a in arrays:
        finished.append(lax.slice_in_dim(whole, at, at + a.shape[along], axis=along))
        at += a.shape[along]
    return tuple(finished)


def laid_out(pieces, dim):
    pieces = jnp.moveaxis(pieces, 0, dim)
    lengths = pieces.shape
    return pieces.reshape(*lengths[:dim], lengths[dim] * lengths[dim + 1], *lengths[dim + 2 :])


def gathered_copies(shard, axis, dim):
    pieces = copy_for_each(shard, axis)
    return laid_out(pieces, dim)


def side_by_side(arrays, axis, dim, along):
    both = jnp.concatenate(arrays, axis=along)
    whole, at, finished = (gathered_copies(both, axis, dim), 0, [])
    for a in arrays:
        finished.append(lax.slice_in_dim(whole, at, at + a.shape[along], axis=along))
        at += a.shape[along]
    return tuple(finished)


def adam_update(factor, moment, square, gradient):
    moment_new = beta_one * moment + (1.0 - beta_one) * gradient
    square_new = beta_two * square + (1.0 - beta_two) * gradient * gradient
    factor_new = factor - learn_rate * (moment_new / first_fix) / (
        jnp.sqrt(square_new / second_fix) + epsilon
    )
    return (factor_new, moment_new, square_new)


def masked(values, block_keep):
    blocks = block_keep.shape[0]
    reshaped_rows = values.reshape(blocks, values.shape[0] // blocks, values.shape[1])
    weighted = reshaped_rows * block_keep.astype(jnp.float32)[:, None, None]
    return weighted.reshape(values.shape).astype(jnp.bfloat16)


def contract_rows(left, right):
    return lax.dot_general(
        left, right, (((0,), (0,)), ((), ())), preferred_element_type=jnp.float32
    )


def contract_cols(left, right):
    return lax.dot_general(
        left, right, (((1,), (1,)), ((), ())), preferred_element_type=jnp.float32
    )


def body(
    activations,
    cotangent,
    block_keep,
    input_factor,
    input_mean,
    input_square,
    output_factor,
    output_mean,
    output_square,
    frozen_base_rows,
    prompts,
):
    input_rows, output_rows = sent_together(
        (input_factor.astype(jnp.bfloat16), output_factor.astype(jnp.bfloat16)),
        ("role", "dp"),
        0,
        1,
    )
    low_input = jnp.dot(activations, input_rows.T, preferred_element_type=jnp.float32)
    low_grad = jnp.dot(cotangent, output_rows.T, preferred_element_type=jnp.float32)
    low_input, low_grad = together((low_input, low_grad), "tp")
    input_kept = masked(low_input, block_keep)
    grad_kept = masked(low_grad, block_keep)
    input_part = contract_rows(grad_kept, activations)
    output_part = contract_rows(input_kept, cotangent)
    group_input, group_output = sent_together_2((input_part, output_part), "role", 0, 1)
    input_sum, output_sum = sent_together_2((group_input, group_output), "dp", 0, 1)
    adapter_factor_scale = adapter_scale / ROLLOUT_TOKENS
    input_new, input_moment, input_second = adam_update(
        input_factor, input_mean, input_square, input_sum * adapter_factor_scale
    )
    output_new, output_moment, output_second = adam_update(
        output_factor, output_mean, output_square, output_sum * adapter_factor_scale
    )
    input_send = input_new.astype(jnp.bfloat16)
    output_send = output_new.astype(jnp.bfloat16)
    adapter_inner_input, inner_output = sent_together((input_send, output_send), "dp", 0, 1)
    input_cols, output_cols = side_by_side((adapter_inner_input, inner_output), "role", 0, 1)
    input_whole, output_whole = (
        gathered_copies(input_cols, "tp", 1),
        gathered_copies(output_cols, "tp", 1),
    )
    rows_here = frozen_base_rows.shape[0]
    row_block = lax.axis_index("dp") * lax.axis_size("tp") + lax.axis_index("tp")
    output_slice = lax.dynamic_slice_in_dim(output_whole, row_block * rows_here, rows_here, 1)
    adapter_delta_rows = contract_rows(output_slice, input_whole)
    merged_weight_rows = (
        frozen_base_rows.astype(jnp.float32) + adapter_scale * adapter_delta_rows
    ).astype(jnp.bfloat16)
    projected = contract_cols(
        merged_weight_rows, lax.all_gather(prompts, ("dp", "tp"), axis=0, tiled=True)
    )
    return (
        input_new,
        output_new,
        input_moment,
        output_moment,
        input_second,
        output_second,
        merged_weight_rows,
        projected.astype(jnp.bfloat16),
    )


def solution(mesh):
    placed = (
        P(("role", "dp"), "tp"),
        P(("role", "dp"), "tp"),
        P(("role", "dp")),
        P(("role", "dp"), "tp"),
        P(("role", "dp"), "tp"),
        P(("role", "dp"), "tp"),
        P(("role", "dp"), "tp"),
        P(("role", "dp"), "tp"),
        P(("role", "dp"), "tp"),
        P(("dp", "tp"), None),
        P(("role", "dp", "tp"), None),
    )
    return jax.shard_map(
        body,
        mesh=mesh,
        in_specs=placed,
        out_specs=(
            P(("role", "dp"), "tp"),
            P(("role", "dp"), "tp"),
            P(("role", "dp"), "tp"),
            P(("role", "dp"), "tp"),
            P(("role", "dp"), "tp"),
            P(("role", "dp"), "tp"),
            P(("dp", "tp"), None),
            P(("dp", "tp"), "role"),
        ),
        check_vma=False,
    )
```

profile of v0, /device:TPU:1, one launch (start us, length us, event | category | flops | bytes accessed | tf_op | source)
XLA Modules:
  0.0 322.9 jit_solution(536169184211410175)
XLA Ops:
  7.2 0.0 copy-start
  7.2 0.8 convert_element_type.37
  8.0 0.7 convert_element_type.38
  8.8 95.1 %all-gather = bf16[64,1,5632]{2,1,0:T(2,128)(2,1)S(1)} all-gather(bf16[1,1,5632]{2,1,0:T(2,128)(2,1)S(1)} %maximum_bitcast_fusion), channel_id=1, replica_groups=mesh['role'=4,'dp'=16,'tp'=4] {'role','dp'}, dimensions={0}, use_global_device_ids=true | all-gather | bytes 732160 | tf_op jit(solution)/shard_map/all_gather | solution.py:24
  103.9 0.1 copy.43
  104.0 0.7 convolution_bitcast_fusion.1
  104.6 0.5 copy-done.1
  105.1 0.4 convolution_bitcast_fusion
  105.5 0.1 copy.29
  105.6 0.1 reshape.75
  105.7 0.1 copy.30
  105.8 0.1 reshape.76
  105.9 1.1 broadcast_in_dim.14
  107.0 4.2 %all-to-all-start = ((f32[4,1,32768]{2,1,0:T(1,128)}), f32[4,1,32768]{2,1,0:T(1,128)S(1)}, u32[]{:S(2)}, u32[]{:S(2)}) async-start(f32[4,1,32768]{2,1,0:T(1,128)} %broadcast_in_dim.14), calls=%async_computation | async-start | bytes 1048576 | tf_op jit(solution)/shard_map/all_to_all | solution.py:29
  111.8 8.5 %all-to-all-done = f32[4,1,32768]{2,1,0:T(1,128)S(1)} async-done(((f32[4,1,32768]{2,1,0:T(1,128)}), f32[4,1,32768]{2,1,0:T(1,128)S(1)}, u32[]{:S(2)}, u32[]{:S(2)}) %all-to-all-start) | async-done | bytes 524320 | tf_op jit(solution)/shard_map/all_to_all | solution.py:29
  120.3 0.5 reduce_sum.29
  120.8 0.1 convert_element_type.41
  120.9 0.1 convert_element_type.43
  121.0 0.3 fusion.10
  121.3 0.5 fusion.11
  121.8 1.2 pad_maximum_fusion
  123.0 6.8 %all-to-all-start.1 = ((f32[4,16,5632]{2,1,0:T(8,128)}), f32[4,16,5632]{2,1,0:T(8,128)S(1)}, u32[]{:S(2)}, u32[]{:S(2)}) async-start(f32[4,16,5632]{2,1,0:T(8,128)} %bitcast.33), calls=%async_computation.1 | async-start | bytes 2883584 | tf_op jit(solution)/shard_map/all_to_all | solution.py:53
  129.8 0.7 all-gather.5.cloned.1.call-update
  130.5 0.0 copy-start.6
  130.6 33.9 %all-to-all-done.1 = f32[4,16,5632]{2,1,0:T(8,128)S(1)} async-done(((f32[4,16,5632]{2,1,0:T(8,128)}), f32[4,16,5632]{2,1,0:T(8,128)S(1)}, u32[]{:S(2)}, u32[]{:S(2)}) %all-to-all-start.1) | async-done | bytes 1441824 | tf_op jit(solution)/shard_map/all_to_all | solution.py:53
  164.5 0.8 reduce_sum.30
  165.4 1.2 reshape.78
  166.6 28.3 %all_to_all.31 = f32[16,1,5632]{2,1,0:T(1,128)S(1)} all-to-all(f32[16,1,5632]{2,1,0:T(1,128)S(1)} %reshape.78), channel_id=1, replica_groups=mesh['role'=4,'dp'=16,'tp'=4] {'dp'}, dimensions={0} | all-to-all | bytes 720896 | tf_op jit(solution)/shard_map/all_to_all | solution.py:53
  194.9 0.2 reduce_sum.31
  195.2 0.7 fusion.8
  195.8 0.7 fusion.9
  196.6 32.9 %all-gather.1 = bf16[16,1,5632]{2,1,0:T(2,128)(2,1)S(1)} all-gather(bf16[1,1,5632]{2,1,0:T(2,128)(2,1)S(1)} %maximum_bitcast_fusion.1), channel_id=1, replica_groups=mesh['role'=4,'dp'=16,'tp'=4] {'dp'}, dimensions={0}, use_global_device_ids=true | all-gather | bytes 191488 | tf_op jit(solution)/shard_map/all_gather | solution.py:24
  229.6 21.0 %all_to_all.32 = bf16[4,16,5632]{2,1,0:T(8,128)(2,1)S(1)} all-to-all(bf16[4,16,5632]{2,1,0:T(8,128)(2,1)S(1)} %broadcast_in_dim.15), channel_id=1, replica_groups=mesh['role'=4,'dp'=16,'tp'=4] {'role'}, dimensions={0} | all-to-all | bytes 1441792 | tf_op jit(solution)/shard_map/all_to_all | solution.py:29
  250.6 0.9 copy-done.4
  251.5 1.1 broadcast_in_dim.17
  252.6 3.5 %all-to-all-start.5 = ((bf16[4,64,2048]{2,1,0:T(8,128)(2,1)}), bf16[4,64,2048]{2,1,0:T(8,128)(2,1)S(1)}, u32[]{:S(2)}, u32[]{:S(2)}) async-start(bf16[4,64,2048]{2,1,0:T(8,128)(2,1)} %broadcast_in_dim.17), calls=%async_computation.5 | async-start | bytes 2097152 | tf_op jit(solution)/shard_map/all_to_all | solution.py:29
  256.1 1.1 slice.48
  257.2 13.1 %all-to-all-done.5 = bf16[4,64,2048]{2,1,0:T(8,128)(2,1)S(1)} async-done(((bf16[4,64,2048]{2,1,0:T(8,128)(2,1)}), bf16[4,64,2048]{2,1,0:T(8,128)(2,1)S(1)}, u32[]{:S(2)}, u32[]{:S(2)}) %all-to-all-start.5) | async-done | bytes 1048608 | tf_op jit(solution)/shard_map/all_to_all | solution.py:29
  270.3 1.5 broadcast_in_dim.16
  271.8 0.1 copy-done.2
  271.9 4.4 %all-to-all-start.4 = ((bf16[4,64,3584]{2,1,0:T(8,128)(2,1)}), bf16[4,64,3584]{2,1,0:T(8,128)(2,1)}, u32[]{:S(2)}, u32[]{:S(2)}) async-start(bf16[4,64,3584]{2,1,0:T(8,128)(2,1)} %broadcast_in_dim.16), calls=%async_computation.4 | async-start | bytes 3670016 | tf_op jit(solution)/shard_map/all_to_all | solution.py:29
  276.3 1.3 copy.40
  277.6 20.5 %all-to-all-done.4 = bf16[4,64,3584]{2,1,0:T(8,128)(2,1)} async-done(((bf16[4,64,3584]{2,1,0:T(8,128)(2,1)}), bf16[4,64,3584]{2,1,0:T(8,128)(2,1)}, u32[]{:S(2)}, u32[]{:S(2)}) %all-to-all-start.4) | async-done | bytes 1835040 | tf_op jit(solution)/shard_map/all_to_all | solution.py:29
  298.1 1.8 copy.39
  299.9 0.8 copy-done.3
  300.7 3.1 fusion.1
  303.7 7.0 %reshape.87 = bf16[256,8192]{1,0:T(8,128)(2,1)} reshape(bf16[64,4,8192]{2,1,0:T(4,128)(2,1)} %all-gather.5.cloned.1.call-done) | data formatting | bytes 8388608
  310.7 5.4 %convolution_convert_fusion = bf16[224,256]{1,0:T(8,128)(2,1)} fusion(bf16[224,8192]{1,0:T(8,128)(2,1)} %fusion.1, bf16[256,8192]{1,0:T(8,128)(2,1)} %reshape.87), kind=kOutput, calls=%fused_computation.4 | convolution fusion | flops 939581440 | bytes 7979008 | tf_op jit(solution)/shard_map/dot_general | solution.py:109
  (26 shorter events, 0.2 us)
Async XLA Ops:
  7.2 96.8 %copy-start = (bf16[256,3584]{1,0:T(8,128)(2,1)S(1)}, bf16[256,3584]{1,0:T(8,128)(2,1)}, u32[]{:S(2)}) copy-start(bf16[256,3584]{1,0:T(8,128)(2,1)} %param.12) | copy-start | bytes 5505028
  103.9 1.2 copy-start.1
  107.0 13.3 %all-to-all-start = ((f32[4,1,32768]{2,1,0:T(1,128)}), f32[4,1,32768]{2,1,0:T(1,128)S(1)}, u32[]{:S(2)}, u32[]{:S(2)}) async-start(f32[4,1,32768]{2,1,0:T(1,128)} %broadcast_in_dim.14), calls=%async_computation | async-start | bytes 1048576 | tf_op jit(solution)/shard_map/all_to_all | solution.py:29
  123.0 41.5 %all-to-all-start.1 = ((f32[4,16,5632]{2,1,0:T(8,128)}), f32[4,16,5632]{2,1,0:T(8,128)S(1)}, u32[]{:S(2)}, u32[]{:S(2)}) async-start(f32[4,16,5632]{2,1,0:T(8,128)} %bitcast.33), calls=%async_computation.1 | async-start | bytes 2883584 | tf_op jit(solution)/shard_map/all_to_all | solution.py:53
  129.8 174.0 %all-gather.5.cloned.1.call-start = ((), (), s32[]{:S(2)}) async-start(), calls=%async_computation.6 | async-start | bytes 4259840 | tf_op jit(solution)/shard_map/all_gather | solution.py:165
  130.5 64.6 %copy-start.6 = (f32[1,2048]{1,0:T(1,128)S(1)}, f32[1,2048]{1,0:T(1,128)}, u32[]{:S(2)}) copy-start(f32[1,2048]{1,0:T(1,128)} %param.14) | copy-start | bytes 24580
  130.5 64.6 %copy-start.9 = (f32[1,2048]{1,0:T(1,128)S(1)}, f32[1,2048]{1,0:T(1,128)}, u32[]{:S(2)}) copy-start(f32[1,2048]{1,0:T(1,128)} %param.15) | copy-start | bytes 24580
  130.5 64.6 %copy-start.10 = (f32[1,2048]{1,0:T(1,128)S(1)}, f32[1,2048]{1,0:T(1,128)}, u32[]{:S(2)}) copy-start(f32[1,2048]{1,0:T(1,128)} %param.16) | copy-start | bytes 24580
  130.5 65.3 %copy-start.5 = (f32[1,3584]{1,0:T(1,128)S(1)}, f32[1,3584]{1,0:T(1,128)}, u32[]{:S(2)}) copy-start(f32[1,3584]{1,0:T(1,128)} %param.17) | copy-start | bytes 43012
  130.6 65.3 %copy-start.7 = (f32[1,3584]{1,0:T(1,128)S(1)}, f32[1,3584]{1,0:T(1,128)}, u32[]{:S(2)}) copy-start(f32[1,3584]{1,0:T(1,128)} %param.18) | copy-start | bytes 43012
  130.6 65.3 %copy-start.8 = (f32[1,3584]{1,0:T(1,128)S(1)}, f32[1,3584]{1,0:T(1,128)}, u32[]{:S(2)}) copy-start(f32[1,3584]{1,0:T(1,128)} %param.19) | copy-start | bytes 43012
  250.6 0.9 copy-start.4
  252.6 17.7 %all-to-all-start.5 = ((bf16[4,64,2048]{2,1,0:T(8,128)(2,1)}), bf16[4,64,2048]{2,1,0:T(8,128)(2,1)S(1)}, u32[]{:S(2)}, u32[]{:S(2)}) async-start(bf16[4,64,2048]{2,1,0:T(8,128)(2,1)} %broadcast_in_dim.17), calls=%async_computation.5 | async-start | bytes 2097152 | tf_op jit(solution)/shard_map/all_to_all | solution.py:29
  270.3 1.6 copy-start.2
  271.9 26.2 %all-to-all-start.4 = ((bf16[4,64,3584]{2,1,0:T(8,128)(2,1)}), bf16[4,64,3584]{2,1,0:T(8,128)(2,1)}, u32[]{:S(2)}, u32[]{:S(2)}) async-start(bf16[4,64,3584]{2,1,0:T(8,128)(2,1)} %broadcast_in_dim.16), calls=%async_computation.4 | async-start | bytes 3670016 | tf_op jit(solution)/shard_map/all_to_all | solution.py:29
  298.1 2.6 copy-start.3
Sparse Core Ops, SparseCore 0:
  134.2 105.8 all-gather.4
where the time goes:
time: 324 us; the launch traced here: 323 us
  blocking collectives  177 us (55%)
  waiting for transfers between devices  76.8 us (24%)
  local copies, waits for them, and re-layouts  18.9 us (6%)
  starting transfers between devices  18.9 us (6%)
  between operations  14.9 us (5%)
  matrix products  10.3 us (3%)
  other arithmetic  5.76 us (2%)
    all_gather x2, blocking collectives, sent_together(): lax.all_gather(both, axis, axis=dim, tiled=True)  128 us
    all_to_all x3, waiting for transfers between devices, copy_for_each(): return lax.all_to_all(copies, axis, split_axis=0, concat_axis=0, tiled=True)  42.1 us
    all_to_all x1, waiting for transfers between devices, summed_on_arrival(): lax.all_to_all(in_blocks(shard, dim, peers), axis, 0, 0, tiled=True)  33.9 us
    all_to_all x1, blocking collectives, summed_on_arrival(): lax.all_to_all(in_blocks(shard, dim, peers), axis, 0, 0, tiled=True)  28.3 us
    all_to_all x1, blocking collectives, copy_for_each(): return lax.all_to_all(copies, axis, split_axis=0, concat_axis=0, tiled=True)  21 us
    all_to_all x3, starting transfers between devices, copy_for_each(): return lax.all_to_all(copies, axis, split_axis=0, concat_axis=0, tiled=True)  12.1 us
    unnamed x25, local copies, waits for them, and re-layouts  9.31 us
    all_to_all x1, starting transfers between devices, summed_on_arrival(): lax.all_to_all(in_blocks(shard, dim, peers), axis, 0, 0, tiled=True)  6.81 us
  transfers between devices with their start and end apart: 5, of which 4 were waited for; matrix products, arithmetic and copies ran while one was open for 4% of the time, Pallas kernels for 0%

commit v1 on v0

v1 whole, which is shorter than its diff:
```python
import jax
import jax.numpy as jnp
from jax import lax
from jax.experimental import pallas as pl
from jax.experimental.pallas import tpu as pltpu
from jax.sharding import PartitionSpec as P

ROLLOUT_TOKENS = 256
RANK = 64
LANES = 128
ROWS_A, ROWS_B = 16, 28
ROWS = ROWS_A + ROWS_B
NX, NY, NZ, NC = 4, 4, 8, 2
BLOCK = 224
WIDE = 256

adapter_scale = 2.0
learn_rate = 0.004
beta_one = 0.9
beta_two = 0.95
epsilon = 1e-08
first_fix = 1.0 - 0.9**20
second_fix = 1.0 - 0.95**20

F32, BF16 = jnp.float32, jnp.bfloat16
MESH = pl.DeviceIdType.MESH


def adam_update(factor, moment, square, gradient):
    moment_new = beta_one * moment + (1.0 - beta_one) * gradient
    square_new = beta_two * square + (1.0 - beta_two) * gradient * gradient
    factor_new = factor - learn_rate * (moment_new / first_fix) / (
        jnp.sqrt(square_new / second_fix) + epsilon
    )
    return (factor_new, moment_new, square_new)


def dot_nn(a, b):
    return lax.dot_general(a, b, (((1,), (0,)), ((), ())), preferred_element_type=F32)


def dot_nt(a, b):
    return lax.dot_general(a, b, (((1,), (1,)), ((), ())), preferred_element_type=F32)


def in_wide_blocks(rows):
    lane = lax.broadcasted_iota(jnp.int32, (1, LANES), 1)
    rolled = {0: rows}
    for off in (32, 64, 96):
        rolled[off] = pltpu.roll(rows, LANES - off, 1)
    out = []
    for k in range(16):
        row, off = divmod(BLOCK * k, LANES)
        turned = rolled[off]
        for half in range(2):
            first = turned[row + half : row + half + 1]
            if off == 0:
                out.append(first)
                continue
            last = min(row + half + 1, ROWS_B - 1)
            second = turned[last : last + 1]
            out.append(jnp.where(lane < LANES - off, first, second))
    return out


def exchange_kernel(
    act_hbm,
    cot_hbm,
    keep_ref,
    fa,
    ma,
    va,
    fb,
    mb,
    vb,
    prompts_hbm,
    grad_out,
    ha,
    bb,
    q,
    act,
    cot,
    g,
    stg8,
    w,
    low,
    stg64,
    p_send,
    r1,
    s2,
    r2,
    t32,
    t16,
    r3,
    ea,
    stga,
    ebz,
    ebx,
    ebd,
    stgb,
    bs,
    pr,
    pf,
    loc,
    ssem,
    rsem,
):
    z_lo = lax.axis_index("role")
    dp = lax.axis_index("dp")
    y = lax.axis_index("tp")
    c = lax.rem(dp, 2)
    x = lax.rem(lax.div(dp, 2), 4)
    zh = lax.div(dp, 8)
    z = zh * 4 + z_lo

    def at(x_=x, y_=y, z_=z, c_=c):
        return {
            "role": lax.rem(z_, 4),
            "dp": lax.div(z_, 4) * 8 + x_ * 2 + c_,
            "tp": y_,
        }

    def step(v, d, n):
        return lax.rem(v + d, n)

    other = 1 - c
    sibling = at(c_=other)
    xs = [step(x, d, NX) for d in range(NX)]
    ys = [step(y, d, NY) for d in range(NY)]
    zs = [step(z, d, NZ) for d in range(NZ)]
    from_x = [step(x, NX - d, NX) for d in range(NX)]
    from_y = [step(y, NY - d, NY) for d in range(NY)]
    from_z = [step(z, NZ - d, NZ) for d in range(NZ)]

    names = {}

    def copy(src, dst, key, device):
        i = names.setdefault(key, len(names))
        return pltpu.make_async_remote_copy(
            src_ref=src,
            dst_ref=dst,
            send_sem=ssem.at[i],
            recv_sem=rsem.at[i],
            device_id=device,
            device_id_type=MESH,
        )

    sent = []

    def send(src, dst, key, device):
        one = copy(src, dst, key, device)
        one.start()
        sent.append(one)

    def arrived(dst, key):
        copy(dst, dst, key, sibling).wait_recv()

    load_act = pltpu.make_async_copy(act_hbm, act, loc.at[0])
    load_cot = pltpu.make_async_copy(cot_hbm, cot, loc.at[1])
    load_act.start()
    load_cot.start()
    quarter = 2048

    def columns(yy):
        return prompts_hbm.at[:, pl.ds(pl.multiple_of(yy * quarter, quarter), quarter)]

    load_own = pltpu.make_async_copy(columns(y), pr.at[y], loc.at[2])
    load_own.start()

    barrier = pltpu.get_barrier_semaphore()
    peers = (
        [sibling]
        + [at(x_=v) for v in xs[1:]]
        + [at(y_=v) for v in ys[1:]]
        + [at(z_=v) for v in zs[1:]]
    )
    for peer in peers:
        pl.semaphore_signal(barrier, inc=1, device_id=peer, device_id_type=MESH)

    g[c, x, z, 0:ROWS_A, :] = fa[...].astype(BF16)
    g[c, x, z, ROWS_A:ROWS, :] = fb[...].astype(BF16)
    pl.semaphore_wait(barrier, len(peers))

    for d in range(1, NZ):
        send(g.at[c, x, z], g.at[c, x, z], ("gz", d), at(z_=zs[d]))
    for d in range(1, NY):
        send(columns(ys[d]), pr.at[y], ("p1", d), at(y_=ys[d]))
    for d in range(1, NZ):
        arrived(g.at[c, x, from_z[d]], ("gz", d))
    for d in range(1, NX):
        send(g.at[c, x], g.at[c, x], ("gx", d), at(x_=xs[d]))
    send(g.at[c, x], g.at[c, x], ("gc", 0), sibling)

    def spread(core, xx):
        stg8[...] = g[core, xx].astype(F32)
        for j in range(ROWS):
            w[core * 4 + xx, :, j * LANES : (j + 1) * LANES] = stg8[:, j, :]

    spread(c, x)

    load_own.wait()
    for d in range(1, NY):
        arrived(pr.at[from_y[d]], ("p1", d))
    for yy in range(NY):
        pf[4 * yy : 4 * yy + 4, :] = pr[yy].astype(F32)
    q[y, zh, x, c] = pf[...].astype(BF16)
    send(q.at[y, zh, x, c], q.at[y, zh, x, c], ("p2", 0), at(z_=step(z, 4, NZ)))

    for d in range(1, NX):
        arrived(g.at[c, from_x[d]], ("gx", d))
        send(g.at[c, from_x[d]], g.at[c, from_x[d]], ("gc", d), sibling)
        spread(c, from_x[d])
    arrived(q.at[y, 1 - zh, x, c], ("p2", 0))
    for d in range(1, NX):
        send(q.at[y, :, x, c], q.at[y, :, x, c], ("p3", d), at(x_=xs[d]))
    for d in range(NX):
        arrived(g.at[other, from_x[d]], ("gc", d))
        spread(other, from_x[d])

    load_act.wait()
    load_cot.wait()
    wide = w[...].reshape(RANK, ROWS * LANES).astype(BF16)
    split = ROWS_A * LANES
    low[y, 0:RANK, :] = dot_nt(wide[:, :split], act[...]).astype(BF16)
    low[y, RANK : 2 * RANK, :] = dot_nt(wide[:, split:], cot[...]).astype(BF16)
    for d in range(1, NY):
        send(low.at[y], low.at[y], ("low", d), at(y_=ys[d]))
    for d in range(1, NY):
        arrived(low.at[from_y[d]], ("low", d))
    total = low[0].astype(F32)
    for yy in range(1, NY):
        total = total + low[yy].astype(F32)
    kept = (total * keep_ref[0].astype(F32)).astype(BF16)
    input_kept, grad_kept = kept[0:RANK], kept[RANK : 2 * RANK]

    chunk = 4
    for i in range(ROWS // chunk):
        first = i * chunk
        if first < ROWS_A:
            part = dot_nn(grad_kept, act[:, first * LANES : (first + chunk) * LANES])
        else:
            at_b = first - ROWS_A
            part = dot_nn(input_kept, cot[:, at_b * LANES : (at_b + chunk) * LANES])
        for j in range(chunk):
            stg64[:, first + j, :] = part[:, j * LANES : (j + 1) * LANES]

    order = [1, 2, 3, 0]
    for d in order:
        rows = pl.ds(other * 32 + xs[d] * 8, 8)
        p_send[d] = stg64[rows].astype(BF16)
        send(p_send.at[d], r1.at[d], ("c1", d), sibling)
    for d in range(1, NX):
        arrived(q.at[y, :, from_x[d], c], ("p3", d))
    for d in range(1, NY):
        send(q.at[y, :, :, c], q.at[y, :, :, c], ("p4", d), at(y_=ys[d]))
    send(q.at[y, :, :, c], q.at[y, :, :, c], ("p5", 0), sibling)
    for d in order:
        arrived(r1.at[d], ("c1", d))
        rows = pl.ds(c * 32 + xs[d] * 8, 8)
        pair = stg64[rows] + r1[d].astype(F32)
        if d:
            s2[d] = pair.astype(BF16)
            send(s2.at[d], r2.at[d], ("c2", d), at(x_=xs[d]))
        else:
            t32[...] = pair
    for d in range(1, NX):
        arrived(r2.at[d], ("c2", d))
    column = t32[...]
    for d in range(1, NX):
        column = column + r2[d].astype(F32)
    t32[...] = column
    t16[...] = column.astype(BF16)
    for d in range(1, NZ):
        send(t16.at[zs[d]], r3.at[d], ("c3", d), at(z_=zs[d]))
    for d in range(1, NZ):
        arrived(r3.at[d], ("c3", d))
    grad = t32[z]
    for d in range(1, NZ):
        grad = grad + r3[d].astype(F32)
    grad = grad * (adapter_scale / ROLLOUT_TOKENS)
    grad_out[...] = grad

    new_a, _, _ = adam_update(fa[...], ma[...], va[...], grad[0:ROWS_A])
    ea[x, z] = new_a.astype(BF16)
    for d in range(1, NZ):
        send(ea.at[x, z], ea.at[x, z], ("ez", d), at(z_=zs[d]))
    new_b, _, _ = adam_update(fb[...], mb[...], vb[...], grad[ROWS_A:ROWS])
    blocks = jnp.concatenate(in_wide_blocks(new_b), axis=0).astype(BF16)
    for kk in range(4):
        ebz[z, kk] = blocks[8 * kk : 8 * kk + 8]
    for d in range(1, NZ):
        send(ebz.at[z], ebz.at[z], ("bz", d), at(z_=zs[d]))
    for d in range(1, NZ):
        arrived(ea.at[x, from_z[d]], ("ez", d))
    for d in range(1, NX):
        send(ea.at[x], ea.at[x], ("ex", d), at(x_=xs[d]))
    for d in range(1, NZ):
        arrived(ebz.at[from_z[d]], ("bz", d))

    def two_blocks(xx):
        return ebz.at[:, pl.ds(lax.rem(xx, 2) * 2, 2)]

    for d in range(1, NX):
        send(two_blocks(xs[d]), ebx.at[x], ("bx", d), at(x_=xs[d]))
    ebx[x] = ebz[:, pl.ds(lax.rem(x, 2) * 2, 2)]
    for d in range(1, NX):
        arrived(ea.at[from_x[d]], ("ex", d))
    for xx in range(NX):
        stga[xx * NZ : (xx + 1) * NZ] = ea[xx].astype(F32)
    for j in range(ROWS_A):
        ha[y, c, :, j * LANES : (j + 1) * LANES] = stga[:, j, :].astype(BF16)
    for d in range(1, NY):
        send(ha.at[y, c], ha.at[y, c], ("ey", d), at(y_=ys[d]))
    send(ha.at[y, c], ha.at[y, c], ("ec", 0), sibling)

    for d in range(1, NY):
        arrived(q.at[from_y[d], :, :, c], ("p4", d))
        send(q.at[from_y[d], :, :, c], q.at[from_y[d], :, :, c], ("p5", d), sibling)

    for d in range(1, NX):
        arrived(ebx.at[from_x[d]], ("bx", d))
    send(ebx.at[:, :, other], ebd, ("bc", 0), sibling)
    for xx in range(NX):
        stgb[c, xx * NZ : (xx + 1) * NZ] = ebx[xx, :, c].astype(F32)
    arrived(ebd, ("bc", 0))
    for xx in range(NX):
        stgb[other, xx * NZ : (xx + 1) * NZ] = ebd[xx].astype(F32)
    for yy in range(NY):
        for cc in range(NC):
            for half in range(2):
                bs[yy, cc, :, half * LANES : (half + 1) * LANES] = stgb[
                    cc, :, 2 * yy + half, :
                ].astype(BF16)
    holder = zh * 2 + lax.div(x, 2)
    for d in range(1, NY):
        key = ("by", d)
        one = copy(bs.at[ys[d]], bb, key, at(y_=ys[d]))

        @pl.when(y == holder)
        def _():
            one.start()

    @pl.when(y == holder)
    def _():
        bb[...] = bs[y]

    for d in range(1, NY):
        arrived(ha.at[from_y[d], c], ("ey", d))
        send(ha.at[from_y[d], c], ha.at[from_y[d], c], ("ec", d), sibling)

    for d in range(1, NY):

        @pl.when(from_y[d] == holder)
        def _():
            arrived(bb, ("by", d))

    for d in range(NY):
        arrived(ha.at[from_y[d], other], ("ec", d))
    for d in range(NY):
        arrived(q.at[from_y[d], :, :, other], ("p5", d))
    for one in sent:
        one.wait_send()

    for d in range(1, NY):
        one = copy(bs.at[ys[d]], bb, ("by", d), at(y_=ys[d]))

        @pl.when(y == holder)
        def _():
            one.wait_send()


SEMAPHORES = 96


def exchange(act, cot, keep, fa, ma, va, fb, mb, vb, prompts):
    any_spec = pl.BlockSpec(memory_space=pl.ANY)
    vmem = pl.BlockSpec(memory_space=pltpu.VMEM)
    smem = pl.BlockSpec(memory_space=pltpu.SMEM)
    tokens = act.shape[0]
    return pl.pallas_call(
        exchange_kernel,
        out_shape=(
            jax.ShapeDtypeStruct((ROWS, LANES), F32),
            jax.ShapeDtypeStruct((NY, NC, 32, 2048), BF16),
            jax.ShapeDtypeStruct((NC, 32, WIDE), BF16),
            jax.ShapeDtypeStruct((NY, 2, NX, NC, 16, 2048), BF16),
        ),
        in_specs=[any_spec, any_spec, smem] + [vmem] * 6 + [any_spec],
        out_specs=(vmem, vmem, vmem, vmem),
        scratch_shapes=[
            pltpu.VMEM(act.shape, BF16),
            pltpu.VMEM(cot.shape, BF16),
            pltpu.VMEM((NC, NX, NZ, ROWS, LANES), BF16),
            pltpu.VMEM((NZ, ROWS, LANES), F32),
            pltpu.VMEM((NC * NX, NZ, ROWS * LANES), F32),
            pltpu.VMEM((NY, 2 * RANK, tokens), BF16),
            pltpu.VMEM((RANK, ROWS, LANES), F32),
            pltpu.VMEM((NX, NZ, ROWS, LANES), BF16),
            pltpu.VMEM((NX, NZ, ROWS, LANES), BF16),
            pltpu.VMEM((NX, NZ, ROWS, LANES), BF16),
            pltpu.VMEM((NX, NZ, ROWS, LANES), BF16),
            pltpu.VMEM((NZ, ROWS, LANES), F32),
            pltpu.VMEM((NZ, ROWS, LANES), BF16),
            pltpu.VMEM((NZ, ROWS, LANES), BF16),
            pltpu.VMEM((NX, NZ, ROWS_A, LANES), BF16),
            pltpu.VMEM((NX * NZ, ROWS_A, LANES), F32),
            pltpu.VMEM((NZ, 4, 8, LANES), BF16),
            pltpu.VMEM((NX, NZ, 2, 8, LANES), BF16),
            pltpu.VMEM((NX, NZ, 8, LANES), BF16),
            pltpu.VMEM((NC, NX * NZ, 8, LANES), F32),
            pltpu.VMEM((NY, NC, 32, WIDE), BF16),
            pltpu.VMEM((NY, 4, 2048), BF16),
            pltpu.VMEM((16, 2048), F32),
            pltpu.SemaphoreType.DMA((3,)),
            pltpu.SemaphoreType.DMA((SEMAPHORES,)),
            pltpu.SemaphoreType.DMA((SEMAPHORES,)),
        ],
        compiler_params=pltpu.CompilerParams(
            collective_id=0, has_side_effects=True, vmem_limit_bytes=32 * 1024 * 1024
        ),
        name="exchange",
    )(act, cot, keep, fa, ma, va, fb, mb, vb, prompts)


def merge_kernel(
    base, ha, bb, q, grad, fa, ma, va, fb, mb, vb, ua, ub, na, nb, sa, sb, merged, proj, bt, acc
):
    i = pl.program_id(0)

    @pl.when(i == 0)
    def _():
        bt[...] = bb[...].reshape(RANK, WIDE).astype(F32).T.astype(BF16)
        ua[...], na[...], sa[...] = adam_update(fa[...], ma[...], va[...], grad[0:ROWS_A])
        ub[...], nb[...], sb[...] = adam_update(fb[...], mb[...], vb[...], grad[ROWS_A:ROWS])

    delta = dot_nn(bt[0:BLOCK, :], ha[0].reshape(RANK, 2048))
    rows = (base[...].astype(F32) + adapter_scale * delta).astype(BF16)
    merged[...] = rows
    part = dot_nt(rows, q[0].reshape(256, 2048))

    @pl.when(i == 0)
    def _():
        acc[...] = part

    @pl.when(i > 0)
    def _():
        acc[...] += part

    @pl.when(i == NY - 1)
    def _():
        proj[...] = acc[...].astype(BF16)


def merge(base, ha, bb, q, grad, fa, ma, va, fb, mb, vb):
    whole = pl.BlockSpec(memory_space=pltpu.VMEM)
    sds = jax.ShapeDtypeStruct

    def fixed(shape):
        return pl.BlockSpec(shape, lambda i: (0,) * len(shape))

    a_shape, b_shape = (ROWS_A, LANES), (ROWS_B, LANES)
    return pl.pallas_call(
        merge_kernel,
        grid=(NY,),
        out_shape=(
            sds(a_shape, F32),
            sds(b_shape, F32),
            sds(a_shape, F32),
            sds(b_shape, F32),
            sds(a_shape, F32),
            sds(b_shape, F32),
            sds(base.shape, BF16),
            sds((BLOCK, 256), BF16),
        ),
        in_specs=[
            pl.BlockSpec((BLOCK, 2048), lambda i: (0, i)),
            pl.BlockSpec((1, NC, 32, 2048), lambda i: (i, 0, 0, 0)),
            fixed((NC, 32, WIDE)),
            pl.BlockSpec((1, 2, NX, NC, 16, 2048), lambda i: (i, 0, 0, 0, 0, 0)),
            fixed((ROWS, LANES)),
        ]
        + [fixed(a_shape)] * 3
        + [fixed(b_shape)] * 3,
        out_specs=[
            fixed(a_shape),
            fixed(b_shape),
            fixed(a_shape),
            fixed(b_shape),
            fixed(a_shape),
            fixed(b_shape),
            pl.BlockSpec((BLOCK, 2048), lambda i: (0, i)),
            fixed((BLOCK, 256)),
        ],
        scratch_shapes=[pltpu.VMEM((WIDE, RANK), BF16), pltpu.VMEM((BLOCK, 256), F32)],
        compiler_params=pltpu.CompilerParams(
            dimension_semantics=("arbitrary",), vmem_limit_bytes=32 * 1024 * 1024
        ),
        name="merge",
    )(base, ha, bb, q, grad, fa, ma, va, fb, mb, vb)


def body(
    activations,
    cotangent,
    block_keep,
    input_factor,
    input_mean,
    input_square,
    output_factor,
    output_mean,
    output_square,
    frozen_base_rows,
    prompts,
):
    fa, ma, va = (v.reshape(ROWS_A, LANES) for v in (input_factor, input_mean, input_square))
    fb, mb, vb = (v.reshape(ROWS_B, LANES) for v in (output_factor, output_mean, output_square))
    grad, ha, bb, q = exchange(
        activations, cotangent, block_keep, fa, ma, va, fb, mb, vb, prompts
    )
    ua, ub, na, nb, sa, sb, merged, projected = merge(
        frozen_base_rows, ha, bb, q, grad, fa, ma, va, fb, mb, vb
    )
    return (
        ua.reshape(1, -1),
        ub.reshape(1, -1),
        na.reshape(1, -1),
        nb.reshape(1, -1),
        sa.reshape(1, -1),
        sb.reshape(1, -1),
        merged,
        projected,
    )


def solution(mesh):
    row = P(("role", "dp"), "tp")
    placed = (
        row,
        row,
        P(("role", "dp")),
        row,
        row,
        row,
        row,
        row,
        row,
        P(("dp", "tp"), None),
        P(("role", "dp", "tp"), None),
    )
    return jax.shard_map(
        body,
        mesh=mesh,
        in_specs=placed,
        out_specs=(
            row,
            row,
            row,
            row,
            row,
            row,
            P(("dp", "tp"), None),
            P(("dp", "tp"), "role"),
        ),
        check_vma=False,
    )
```

time: 324 us -> 84.2 us (0.26)
  blocking collectives: 177 us -> 0 us
  waiting for transfers between devices: 76.8 us -> 0 us
  Pallas kernels: 0 us -> 68.8 us
  starting transfers between devices: 18.9 us -> 0 us
  between operations: 14.9 us -> 1.32 us
  matrix products: 10.3 us -> 0 us
  local copies, waits for them, and re-layouts: 18.9 us -> 11 us
  other arithmetic: 5.76 us -> 2.26 us
    all_gather x2 -> x0, blocking collectives: 128 us -> none  [sent_together(): lax.all_gather(both, axis, axis=dim, tiled=True)]
    all_to_all x4 -> x0, waiting for transfers between devices: 76.1 us -> none  [the longest x3 42.1 us: copy_for_each(): return lax.all_to_all(copies, axis, split_axis=0, concat_axis=0, tiled=True)]
    pallas_call x0 -> x2, Pallas kernels: none -> 68.8 us  [the longest x1 64.3 us: exchange(): pl.pallas_call(exchange_kernel, out_shape=(jax.ShapeDtypeStruct((ROWS, LA...]
    all_to_all x2 -> x0, blocking collectives: 49.3 us -> none  [the longest x1 28.3 us: summed_on_arrival(): lax.all_to_all(in_blocks(shard, dim, peers), axis, 0, 0, tiled=True)]
    all_to_all x4 -> x0, starting transfers between devices: 18.9 us -> none  [the longest x3 12.1 us: copy_for_each(): return lax.all_to_all(copies, axis, split_axis=0, concat_axis=0, tiled=True)]
    dot_general x6 -> x0, matrix products: 10.3 us -> none  [the longest x1 5.35 us: contract_cols(): lax.dot_general(left, right, (((1,), (1,)), ((), ())), preferred_element_...]
    reshape x5 -> x1, local copies, waits for them, and re-layouts: 4.5 us -> 0.63 us  [body(): sb.reshape(1, -1)]
    broadcast_in_dim x4 -> x0, local copies, waits for them, and re-layouts: 3.69 us -> none  [copy_for_each(): copies = jnp.broadcast_to(shard, (lax.axis_size(axis), *shard.shape))]
  transfers between devices with their start and end apart: 5 -> 0, of which waited for: 4 -> 0; matrix products, arithmetic and copies ran while one was open for 4% -> 0% of each run, Pallas kernels for 0% -> 0%
where the time goes in v1:
time: 84.2 us; the launch traced here: 83.4 us
  Pallas kernels  68.8 us (82%)
  local copies, waits for them, and re-layouts  11 us (13%)
  other arithmetic  2.26 us (3%)
  between operations  1.32 us (2%)
    pallas_call x1, Pallas kernels, exchange(): pl.pallas_call(exchange_kernel, out_shape=(jax.ShapeDtypeStruct((ROWS, LA...  64.3 us
    unnamed x21, local copies, waits for them, and re-layouts  10.4 us
    pallas_call x1, Pallas kernels, merge(): pl.pallas_call(merge_kernel, grid=(NY,), out_shape=(sds(a_shape, F32), sd...  4.59 us
    unnamed x3, other arithmetic  2.26 us

profile of v1, /device:TPU:1, one launch (start us, length us, event | category | flops | bytes accessed | tf_op | source)
XLA Modules:
  0.0 83.4 jit_solution(16896656816853714806)
XLA Ops:
  1.3 0.8 reduce
  2.0 0.8 reduce.1
  2.8 0.8 reduce.2
  3.5 0.0 copy-start.1
  3.6 1.5 %copy-done.1 = bf16[256,3584]{1,0:T(8,128)(2,1)S(1)} copy-done((bf16[256,3584]{1,0:T(8,128)(2,1)S(1)}, bf16[256,3584]{1,0:T(8,128)(2,1)}, u32[]{:S(2)}) %copy-start.1) | copy-done | bytes 1835032
  5.0 0.0 copy-start.2
  5.1 1.2 %copy-done.2 = bf16[256,2048]{1,0:T(8,128)(2,1)S(1)} copy-done((bf16[256,2048]{1,0:T(8,128)(2,1)S(1)}, bf16[256,2048]{1,0:T(8,128)(2,1)}, u32[]{:S(2)}) %copy-start.2) | copy-done | bytes 1048600
  6.3 0.0 copy-start.3
  6.3 0.8 %copy-done.3 = bf16[4,8192]{1,0:T(4,128)(2,1)S(1)} copy-done((bf16[4,8192]{1,0:T(4,128)(2,1)S(1)}, bf16[4,8192]{1,0:T(4,128)(2,1)}, u32[]{:S(2)}) %copy-start.3) | copy-done | bytes 65560
  7.1 0.0 copy-start.4
  7.1 0.7 copy-done.4
  7.8 0.0 copy-start.6
  7.8 0.7 copy-done.6
  8.5 0.0 copy-start.8
  8.5 0.7 copy-done.8
  9.2 64.3 %exchange.1 = (f32[44,128]{1,0:T(8,128)S(1)}, bf16[4,2,32,2048]{3,2,1,0:T(8,128)(2,1)S(1)}, bf16[2,32,256]{2,1,0:T(8,128)(2,1)S(1)}, bf16[4,2,4,2,16,2048]{5,4,3,2,1,0:T(8,128)(2,1)S(1)}) custom-call(bf16[256,2048]{1,0:T(8,128)(2,1)S(1)} %copy-done.2, bf16[256,3584]{1,0:T(8,128)(2,1)S(1)} %copy-done.1, s32[1]{0:T(128)S(6)} %copy.26.keep_ref, ...), custom_call_target="tpu_custom_call" | custom-call | tf_op jit(solution)/shard_map/exchange/pallas_call | solution.py:380
  73.5 0.0 copy-start
  73.5 2.0 %copy-done = bf16[224,8192]{1,0:T(8,128)(2,1)S(1)} copy-done((bf16[224,8192]{1,0:T(8,128)(2,1)S(1)}, bf16[224,8192]{1,0:T(8,128)(2,1)}, u32[]{:S(2)}) %copy-start) | copy-done | bytes 3670040
  75.5 0.0 copy-start.5
  75.5 0.7 copy-done.5
  76.2 0.0 copy-start.7
  76.2 0.7 copy-done.7
  76.9 0.0 copy-start.9
  76.9 0.7 copy-done.9
  77.6 4.6 %merge.1 = (f32[16,128]{1,0:T(8,128)}, f32[28,128]{1,0:T(8,128)S(1)}, f32[16,128]{1,0:T(8,128)}, f32[28,128]{1,0:T(8,128)S(1)}, f32[16,128]{1,0:T(8,128)}, /*ind...) custom-call(bf16[224,8192]{1,0:T(8,128)(2,1)S(1)} %copy-done, ...), custom_call_target="tpu_custom_call" | custom-call | tf_op jit(solution)/shard_map/merge/pallas_call | solution.py:462
  82.2 0.6 copy.25
  82.8 0.6 copy_bitcast_fusion
Async XLA Ops:
  3.5 1.5 %copy-start.1 = (bf16[256,3584]{1,0:T(8,128)(2,1)S(1)}, bf16[256,3584]{1,0:T(8,128)(2,1)}, u32[]{:S(2)}) copy-start(bf16[256,3584]{1,0:T(8,128)(2,1)} %cot_hbm.1) | copy-start | bytes 5505028
  5.0 1.2 %copy-start.2 = (bf16[256,2048]{1,0:T(8,128)(2,1)S(1)}, bf16[256,2048]{1,0:T(8,128)(2,1)}, u32[]{:S(2)}) copy-start(bf16[256,2048]{1,0:T(8,128)(2,1)} %act_hbm.1) | copy-start | bytes 3145732
  6.3 0.8 %copy-start.3 = (bf16[4,8192]{1,0:T(4,128)(2,1)S(1)}, bf16[4,8192]{1,0:T(4,128)(2,1)}, u32[]{:S(2)}) copy-start(bf16[4,8192]{1,0:T(4,128)(2,1)} %prompts_hbm.1) | copy-start | bytes 196612
  7.1 0.7 copy-start.4
  7.8 0.7 copy-start.6
  8.5 0.7 copy-start.8
  73.5 2.0 %copy-start = (bf16[224,8192]{1,0:T(8,128)(2,1)S(1)}, bf16[224,8192]{1,0:T(8,128)(2,1)}, u32[]{:S(2)}) copy-start(bf16[224,8192]{1,0:T(8,128)(2,1)} %base.1) | copy-start | bytes 11010052
  75.5 0.7 copy-start.5
  76.2 0.7 copy-start.7
  76.9 0.7 copy-start.9

commit v2 on v1

--- a/solution.py
+++ b/solution.py
@@ -67,12 +67,12 @@
     act_hbm,
     cot_hbm,
     keep_ref,
-    fa,
-    ma,
-    va,
-    fb,
-    mb,
-    vb,
+    fa_hbm,
+    ma_hbm,
+    va_hbm,
+    fb_hbm,
+    mb_hbm,
+    vb_hbm,
     prompts_hbm,
     grad_out,
     ha,
@@ -80,6 +80,12 @@
     q,
     act,
     cot,
+    fa,
+    ma,
+    va,
+    fb,
+    mb,
+    vb,
     g,
     stg8,
     w,
@@ -157,15 +163,25 @@
 
     load_act = pltpu.make_async_copy(act_hbm, act, loc.at[0])
     load_cot = pltpu.make_async_copy(cot_hbm, cot, loc.at[1])
+    loads = [
+        pltpu.make_async_copy(src, dst, loc.at[3 + i])
+        for i, (src, dst) in enumerate(
+            ((fa_hbm, fa), (fb_hbm, fb), (ma_hbm, ma), (va_hbm, va), (mb_hbm, mb), (vb_hbm, vb))
+        )
+    ]
+    for one in loads[:2]:
+        one.start()
+    quarter = 2048
+
+    def columns(yy):
+        return prompts_hbm.at[:, pl.ds(pl.multiple_of(yy * quarter, quarter), quarter)]
+
+    load_own = pltpu.make_async_copy(columns(y), pr.at[y], loc.at[2])
+    load_own.start()
     load_act.start()
     load_cot.start()
-    quarter = 2048
-
-    def columns(yy):
-        return prompts_hbm.at[:, pl.ds(pl.multiple_of(yy * quarter, quarter), quarter)]
-
-    load_own = pltpu.make_async_copy(columns(y), pr.at[y], loc.at[2])
-    load_own.start()
+    for one in loads[2:]:
+        one.start()
 
     barrier = pltpu.get_barrier_semaphore()
     peers = (
@@ -177,8 +193,10 @@
     for peer in peers:
         pl.semaphore_signal(barrier, inc=1, device_id=peer, device_id_type=MESH)
 
-    g[c, x, z, 0:ROWS_A, :] = fa[...].astype(BF16)
-    g[c, x, z, ROWS_A:ROWS, :] = fb[...].astype(BF16)
+    for one in loads[:2]:
+        one.wait()
+    g[c, x, z, 0:ROWS_A, :] = fa[:, 0, :].astype(BF16)
+    g[c, x, z, ROWS_A:ROWS, :] = fb[:, 0, :].astype(BF16)
     pl.semaphore_wait(barrier, len(peers))
 
     for d in range(1, NZ):
@@ -219,6 +237,8 @@
 
     load_act.wait()
     load_cot.wait()
+    for one in loads[2:]:
+        one.wait()
     wide = w[...].reshape(RANK, ROWS * LANES).astype(BF16)
     split = ROWS_A * LANES
     low[y, 0:RANK, :] = dot_nt(wide[:, :split], act[...]).astype(BF16)
@@ -280,11 +300,11 @@
     grad = grad * (adapter_scale / ROLLOUT_TOKENS)
     grad_out[...] = grad
 
-    new_a, _, _ = adam_update(fa[...], ma[...], va[...], grad[0:ROWS_A])
+    new_a, _, _ = adam_update(fa[:, 0, :], ma[:, 0, :], va[:, 0, :], grad[0:ROWS_A])
     ea[x, z] = new_a.astype(BF16)
     for d in range(1, NZ):
         send(ea.at[x, z], ea.at[x, z], ("ez", d), at(z_=zs[d]))
-    new_b, _, _ = adam_update(fb[...], mb[...], vb[...], grad[ROWS_A:ROWS])
+    new_b, _, _ = adam_update(fb[:, 0, :], mb[:, 0, :], vb[:, 0, :], grad[ROWS_A:ROWS])
     blocks = jnp.concatenate(in_wide_blocks(new_b), axis=0).astype(BF16)
     for kk in range(4):
         ebz[z, kk] = blocks[8 * kk : 8 * kk + 8]
@@ -372,8 +392,12 @@
 SEMAPHORES = 96
 
 
+def in_hbm(array):
+    return pltpu.with_memory_space_constraint(array, pltpu.HBM)
+
+
 def exchange(act, cot, keep, fa, ma, va, fb, mb, vb, prompts):
-    any_spec = pl.BlockSpec(memory_space=pl.ANY)
+    hbm = pl.BlockSpec(memory_space=pltpu.HBM)
     vmem = pl.BlockSpec(memory_space=pltpu.VMEM)
     smem = pl.BlockSpec(memory_space=pltpu.SMEM)
     tokens = act.shape[0]
@@ -385,11 +409,17 @@
             jax.ShapeDtypeStruct((NC, 32, WIDE), BF16),
             jax.ShapeDtypeStruct((NY, 2, NX, NC, 16, 2048), BF16),
         ),
-        in_specs=[any_spec, any_spec, smem] + [vmem] * 6 + [any_spec],
+        in_specs=[hbm, hbm, smem] + [hbm] * 7,
         out_specs=(vmem, vmem, vmem, vmem),
         scratch_shapes=[
             pltpu.VMEM(act.shape, BF16),
             pltpu.VMEM(cot.shape, BF16),
+            pltpu.VMEM(fa.shape, F32),
+            pltpu.VMEM(fa.shape, F32),
+            pltpu.VMEM(fa.shape, F32),
+            pltpu.VMEM(fb.shape, F32),
+            pltpu.VMEM(fb.shape, F32),
+            pltpu.VMEM(fb.shape, F32),
             pltpu.VMEM((NC, NX, NZ, ROWS, LANES), BF16),
             pltpu.VMEM((NZ, ROWS, LANES), F32),
             pltpu.VMEM((NC * NX, NZ, ROWS * LANES), F32),
@@ -411,15 +441,18 @@
             pltpu.VMEM((NY, NC, 32, WIDE), BF16),
             pltpu.VMEM((NY, 4, 2048), BF16),
             pltpu.VMEM((16, 2048), F32),
-            pltpu.SemaphoreType.DMA((3,)),
+            pltpu.SemaphoreType.DMA((9,)),
             pltpu.SemaphoreType.DMA((SEMAPHORES,)),
             pltpu.SemaphoreType.DMA((SEMAPHORES,)),
         ],
         compiler_params=pltpu.CompilerParams(
             collective_id=0, has_side_effects=True, vmem_limit_bytes=32 * 1024 * 1024
         ),
+        cost_estimate=pl.CostEstimate(
+            flops=200_000_000_000, bytes_accessed=8_000_000, transcendentals=0
+        ),
         name="exchange",
-    )(act, cot, keep, fa, ma, va, fb, mb, vb, prompts)
+    )(in_hbm(act), in_hbm(cot), keep, *map(in_hbm, (fa, ma, va, fb, mb, vb)), in_hbm(prompts))
 
 
 def merge_kernel(
@@ -430,8 +463,12 @@
     @pl.when(i == 0)
     def _():
         bt[...] = bb[...].reshape(RANK, WIDE).astype(F32).T.astype(BF16)
-        ua[...], na[...], sa[...] = adam_update(fa[...], ma[...], va[...], grad[0:ROWS_A])
-        ub[...], nb[...], sb[...] = adam_update(fb[...], mb[...], vb[...], grad[ROWS_A:ROWS])
+        ua[:, 0, :], na[:, 0, :], sa[:, 0, :] = adam_update(
+            fa[:, 0, :], ma[:, 0, :], va[:, 0, :], grad[0:ROWS_A]
+        )
+        ub[:, 0, :], nb[:, 0, :], sb[:, 0, :] = adam_update(
+            fb[:, 0, :], mb[:, 0, :], vb[:, 0, :], grad[ROWS_A:ROWS]
+        )
 
     delta = dot_nn(bt[0:BLOCK, :], ha[0].reshape(RANK, 2048))
     rows = (base[...].astype(F32) + adapter_scale * delta).astype(BF16)
@@ -458,7 +495,7 @@
     def fixed(shape):
         return pl.BlockSpec(shape, lambda i: (0,) * len(shape))
 
-    a_shape, b_shape = (ROWS_A, LANES), (ROWS_B, LANES)
+    a_shape, b_shape = (ROWS_A, 1, LANES), (ROWS_B, 1, LANES)
     return pl.pallas_call(
         merge_kernel,
         grid=(NY,),
@@ -512,8 +549,8 @@
     frozen_base_rows,
     prompts,
 ):
-    fa, ma, va = (v.reshape(ROWS_A, LANES) for v in (input_factor, input_mean, input_square))
-    fb, mb, vb = (v.reshape(ROWS_B, LANES) for v in (output_factor, output_mean, output_square))
+    fa, ma, va = (v.reshape(ROWS_A, 1, LANES) for v in (input_factor, input_mean, input_square))
+    fb, mb, vb = (v.reshape(ROWS_B, 1, LANES) for v in (output_factor, output_mean, output_square))
     grad, ha, bb, q = exchange(
         activations, cotangent, block_keep, fa, ma, va, fb, mb, vb, prompts
     )

time: 84.2 us -> 70.5 us (0.84)
  local copies, waits for them, and re-layouts: 11 us -> 0.03 us
  other arithmetic: 2.26 us -> 0 us
    unnamed x21 -> x14, local copies, waits for them, and re-layouts: 10.4 us -> 0.03 us
    unnamed x3 -> x0, other arithmetic: 2.26 us -> none
where the time goes in v2:
time: 70.5 us; the launch traced here: 70.4 us
  Pallas kernels  69 us (98%)
  between operations  1.4 us (2%)
    pallas_call x1, Pallas kernels, exchange(): pl.pallas_call(exchange_kernel, out_shape=(jax.ShapeDtypeStruct((ROWS, LA...  64.3 us
    pallas_call x1, Pallas kernels, merge(): pl.pallas_call(merge_kernel, grid=(NY,), out_shape=(sds(a_shape, F32), sd...  4.69 us

profile of v2, /device:TPU:1, one launch (start us, length us, event | category | flops | bytes accessed | tf_op | source)
XLA Modules:
  0.0 70.4 jit_solution(9499392992145335548)
XLA Ops:
  1.3 0.0 copy-start
  1.3 0.0 copy-start.1
  1.3 0.0 copy-start.2
  1.3 0.0 copy-start.3
  1.3 0.0 copy-start.4
  1.3 0.0 copy-start.5
  1.3 0.0 copy-start.6
  1.4 64.3 %exchange.1 = (f32[44,128]{1,0:T(8,128)S(1)}, bf16[4,2,32,2048]{3,2,1,0:T(8,128)(2,1)S(1)}, bf16[2,32,256]{2,1,0:T(8,128)(2,1)S(1)}, bf16[4,2,4,2,16,2048]{5,4,3,2,1,0:T(8,128)(2,1)S(1)}) custom-call(bf16[256,2048]{1,0:T(8,128)(2,1)} %act_hbm.1, bf16[256,3584]{1,0:T(8,128)(2,1)} %cot_hbm.1, s32[1]{0:T(128)S(6)} %copy.19.keep_ref, f32[16,1,128]{2,1,0:T(1,128)} %bitcast.18, ...), custom_call_target="tpu_custom_call" | custom-call | flops 199999995904 | bytes 8000000 | tf_op jit(solution)/shard_map/exchange/pallas_call | solution.py:404
  65.7 0.0 copy-done
  65.7 0.0 copy-done.1
  65.7 0.0 copy-done.2
  65.7 0.0 copy-done.3
  65.7 0.0 copy-done.4
  65.7 0.0 copy-done.5
  65.7 0.0 copy-done.6
  65.7 4.7 %merge.1 = (f32[16,1,128]{2,1,0:T(1,128)}, f32[28,1,128]{2,1,0:T(1,128)}, f32[16,1,128]{2,1,0:T(1,128)}, f32[28,1,128]{2,1,0:T(1,128)}, f32[16,1,128]{2,1,0:T(1,...) custom-call(bf16[224,8192]{1,0:T(8,128)(2,1)S(1)} %copy-done, ...), custom_call_target="tpu_custom_call" | custom-call | tf_op jit(solution)/shard_map/merge/pallas_call | solution.py:499
Async XLA Ops:
  1.3 64.4 %copy-start = (bf16[224,8192]{1,0:T(8,128)(2,1)S(1)}, bf16[224,8192]{1,0:T(8,128)(2,1)}, u32[]{:S(2)}) copy-start(bf16[224,8192]{1,0:T(8,128)(2,1)} %base.1) | copy-start | bytes 11010052
  1.3 64.4 %copy-start.1 = (f32[1,3584]{1,0:T(1,128)S(1)}, f32[1,3584]{1,0:T(1,128)}, u32[]{:S(2)}) copy-start(f32[1,3584]{1,0:T(1,128)} %param.17) | copy-start | bytes 43012
  1.3 64.4 %copy-start.2 = (f32[1,3584]{1,0:T(1,128)S(1)}, f32[1,3584]{1,0:T(1,128)}, u32[]{:S(2)}) copy-start(f32[1,3584]{1,0:T(1,128)} %param.18) | copy-start | bytes 43012
  1.3 64.4 %copy-start.3 = (f32[1,3584]{1,0:T(1,128)S(1)}, f32[1,3584]{1,0:T(1,128)}, u32[]{:S(2)}) copy-start(f32[1,3584]{1,0:T(1,128)} %param.19) | copy-start | bytes 43012
  1.3 64.4 %copy-start.4 = (f32[1,2048]{1,0:T(1,128)S(1)}, f32[1,2048]{1,0:T(1,128)}, u32[]{:S(2)}) copy-start(f32[1,2048]{1,0:T(1,128)} %param.14) | copy-start | bytes 24580
  1.3 64.4 %copy-start.5 = (f32[1,2048]{1,0:T(1,128)S(1)}, f32[1,2048]{1,0:T(1,128)}, u32[]{:S(2)}) copy-start(f32[1,2048]{1,0:T(1,128)} %param.15) | copy-start | bytes 24580
  1.3 64.4 %copy-start.6 = (f32[1,2048]{1,0:T(1,128)S(1)}, f32[1,2048]{1,0:T(1,128)}, u32[]{:S(2)}) copy-start(f32[1,2048]{1,0:T(1,128)} %param.16) | copy-start | bytes 24580

commit v3 on v2

v3 whole, which is shorter than its diff:
```python
import jax
import jax.numpy as jnp
from jax import lax
from jax.experimental import pallas as pl
from jax.experimental.pallas import tpu as pltpu
from jax.sharding import PartitionSpec as P

ROLLOUT_TOKENS = 256
RANK = 64
LANES = 128
ROWS_A, ROWS_B = 16, 28
ROWS = ROWS_A + ROWS_B
NX, NY, NZ, NC = 4, 4, 8, 2
BLOCK = 224
WIDE = 256
HALF, PART = 4096, 1024

adapter_scale = 2.0
learn_rate = 0.004
beta_one = 0.9
beta_two = 0.95
epsilon = 1e-08
first_fix = 1.0 - 0.9**20
second_fix = 1.0 - 0.95**20

F32, BF16 = jnp.float32, jnp.bfloat16
MESH = pl.DeviceIdType.MESH


def adam_update(factor, moment, square, gradient):
    moment_new = beta_one * moment + (1.0 - beta_one) * gradient
    square_new = beta_two * square + (1.0 - beta_two) * gradient * gradient
    factor_new = factor - learn_rate * (moment_new / first_fix) / (
        jnp.sqrt(square_new / second_fix) + epsilon
    )
    return (factor_new, moment_new, square_new)


def dot_nn(a, b):
    return lax.dot_general(a, b, (((1,), (0,)), ((), ())), preferred_element_type=F32)


def dot_nt(a, b):
    return lax.dot_general(a, b, (((1,), (1,)), ((), ())), preferred_element_type=F32)


def in_wide_blocks(rows):
    lane = lax.broadcasted_iota(jnp.int32, (1, LANES), 1)
    rolled = {0: rows}
    for off in (32, 64, 96):
        rolled[off] = pltpu.roll(rows, LANES - off, 1)
    out = []
    for k in range(16):
        row, off = divmod(BLOCK * k, LANES)
        turned = rolled[off]
        for half in range(2):
            first = turned[row + half : row + half + 1]
            if off == 0:
                out.append(first)
                continue
            last = min(row + half + 1, ROWS_B - 1)
            second = turned[last : last + 1]
            out.append(jnp.where(lane < LANES - off, first, second))
    return out


def exchange_kernel(
    act_hbm,
    cot_hbm,
    keep_ref,
    fa_hbm,
    ma_hbm,
    va_hbm,
    fb_hbm,
    mb_hbm,
    vb_hbm,
    prompts_hbm,
    base_hbm,
    grad_out,
    ha0,
    ha1,
    bb,
    part_out,
    q1,
    q2,
    base,
    act,
    cot,
    fa,
    ma,
    va,
    fb,
    mb,
    vb,
    ga,
    gb,
    stg32,
    stg8,
    wa,
    wb,
    low,
    sa,
    sb,
    pa,
    pb,
    r1a,
    r1b,
    f2a,
    s2a,
    s2b,
    r2a,
    r2b,
    t32a,
    t32b,
    t16a,
    t16b,
    r3a,
    r3b,
    ez,
    ea0,
    ea1,
    stga,
    stgy,
    ebz,
    ebx,
    ebd,
    stgb,
    bs,
    pr1,
    pr2,
    pf1,
    pf2,
    loc,
    ssem,
    rsem,
):
    z_lo = lax.axis_index("role")
    dp = lax.axis_index("dp")
    y = lax.axis_index("tp")
    c = lax.rem(dp, 2)
    x = lax.rem(lax.div(dp, 2), 4)
    zh = lax.div(dp, 8)
    z = zh * 4 + z_lo

    def at(x_=x, y_=y, z_=z, c_=c):
        return {
            "role": lax.rem(z_, 4),
            "dp": lax.div(z_, 4) * 8 + x_ * 2 + c_,
            "tp": y_,
        }

    def step(v, d, n):
        return lax.rem(v + d, n)

    other = 1 - c
    sibling = at(c_=other)
    xs = [step(x, d, NX) for d in range(NX)]
    ys = [step(y, d, NY) for d in range(NY)]
    zs = [step(z, d, NZ) for d in range(NZ)]
    from_x = [step(x, NX - d, NX) for d in range(NX)]
    from_y = [step(y, NY - d, NY) for d in range(NY)]
    from_z = [step(z, NZ - d, NZ) for d in range(NZ)]

    names = {}

    def copy(src, dst, key, device):
        i = names.setdefault(key, len(names))
        return pltpu.make_async_remote_copy(
            src_ref=src,
            dst_ref=dst,
            send_sem=ssem.at[i],
            recv_sem=rsem.at[i],
            device_id=device,
            device_id_type=MESH,
        )

    sent = []

    def send(src, dst, key, device):
        one = copy(src, dst, key, device)
        one.start()
        sent.append((key[0], None, one))

    def drain(*kinds):
        for name, condition, one in [e for e in sent if not kinds or e[0] in kinds]:
            if condition is None:
                one.wait_send()
            else:
                pl.when(condition)(one.wait_send)
        sent[:] = [e for e in sent if kinds and e[0] not in kinds]

    def arrived(dst, key):
        copy(dst, dst, key, sibling).wait_recv()

    load_act = pltpu.make_async_copy(act_hbm, act, loc.at[0])
    load_cot = pltpu.make_async_copy(cot_hbm, cot, loc.at[1])
    loads = [
        pltpu.make_async_copy(src, dst, loc.at[3 + i])
        for i, (src, dst) in enumerate(
            ((fa_hbm, fa), (fb_hbm, fb), (ma_hbm, ma), (va_hbm, va), (mb_hbm, mb), (vb_hbm, vb))
        )
    ]
    for one in loads[:2]:
        one.start()

    def late(yy):
        return prompts_hbm.at[:, pl.ds(pl.multiple_of(HALF + yy * PART, PART), PART)]

    early = prompts_hbm.at[:, 0:HALF]
    load_early = pltpu.make_async_copy(early, pr1.at[y], loc.at[2])
    load_late = pltpu.make_async_copy(late(y), pr2.at[y], loc.at[9])
    load_base = pltpu.make_async_copy(base_hbm, base, loc.at[10])
    load_early.start()
    load_late.start()
    load_act.start()
    load_cot.start()
    for one in loads[2:]:
        one.start()
    load_base.start()

    barrier = pltpu.get_barrier_semaphore()
    peers = (
        [sibling]
        + [at(x_=v) for v in xs[1:]]
        + [at(y_=v) for v in ys[1:]]
        + [at(z_=v) for v in zs[1:]]
    )
    for peer in peers:
        pl.semaphore_signal(barrier, inc=1, device_id=peer, device_id_type=MESH)

    for one in loads[:2]:
        one.wait()
    ga[c, x, z] = fa[:, 0, :].astype(BF16)
    gb[c, x, z] = fb[:, 0, :].astype(BF16)
    pl.semaphore_wait(barrier, len(peers))

    for d in range(1, NX):
        send(ga.at[c, x, z], ga.at[c, x, z], ("gax", d), at(x_=xs[d]))
    for d in range(1, NZ):
        send(gb.at[c, x, z], gb.at[c, x, z], ("gbz", d), at(z_=zs[d]))
    for d in range(1, NY):
        send(late(ys[d]), pr2.at[y], ("p1b", d), at(y_=ys[d]))
    for d in range(1, NY):
        send(early, pr1.at[y], ("p1a", d), at(y_=ys[d]))
    for d in range(1, NX):
        arrived(ga.at[c, from_x[d], z], ("gax", d))
    for d in range(1, NZ):
        send(ga.at[c, :, z], ga.at[c, :, z], ("gaz", d), at(z_=zs[d]))
    for d in range(1, NZ):
        arrived(gb.at[c, x, from_z[d]], ("gbz", d))
    for d in range(1, NX):
        send(gb.at[c, x], gb.at[c, x], ("gbx", d), at(x_=xs[d]))
    send(gb.at[c, x], gb.at[c, x], ("gbc", 0), sibling)

    def spread_a(core):
        stg32[...] = ga[core].reshape(32, ROWS_A, LANES).astype(F32)
        for j in range(ROWS_A):
            wa[core, :, j * LANES : (j + 1) * LANES] = stg32[:, j, :]

    def spread_b(core, xx):
        stg8[...] = gb[core, xx].astype(F32)
        for j in range(ROWS_B):
            wb[core * 4 + xx, :, j * LANES : (j + 1) * LANES] = stg8[:, j, :]

    spread_b(c, x)

    z_pair = at(z_=step(z, 4, NZ))
    load_late.wait()
    for d in range(1, NY):
        arrived(pr2.at[from_y[d]], ("p1b", d))
    for yy in range(NY):
        pf2[4 * yy : 4 * yy + 4, :] = pr2[yy].astype(F32)
    q2[y, zh, x, c] = pf2[...].astype(BF16)
    load_early.wait()
    for d in range(1, NY):
        arrived(pr1.at[from_y[d]], ("p1a", d))
    for yy in range(NY):
        pf1[4 * yy : 4 * yy + 4, :] = pr1[yy].astype(F32)
    q1[zh, x, c] = pf1[...].astype(BF16)

    for d in range(1, NZ):
        arrived(ga.at[c, :, from_z[d]], ("gaz", d))
    send(ga.at[c], ga.at[c], ("gac", 0), sibling)
    send(q2.at[y, zh, x, c], q2.at[y, zh, x, c], ("p2b", 0), z_pair)
    spread_a(c)
    for d in range(1, NX):
        arrived(gb.at[c, from_x[d]], ("gbx", d))
        send(gb.at[c, from_x[d]], gb.at[c, from_x[d]], ("gbc", d), sibling)
        spread_b(c, from_x[d])
    arrived(ga.at[other], ("gac", 0))
    send(q1.at[zh, x, c], q1.at[zh, x, c], ("p2a", 0), z_pair)
    spread_a(other)
    for d in range(NX):
        arrived(gb.at[other, from_x[d]], ("gbc", d))
        spread_b(other, from_x[d])

    load_act.wait()
    load_cot.wait()
    for one in loads[2:]:
        one.wait()
    wide_a = wa[...].reshape(RANK, ROWS_A * LANES).astype(BF16)
    wide_b = wb[...].reshape(RANK, ROWS_B * LANES).astype(BF16)
    low[y, 0:RANK, :] = dot_nt(wide_a, act[...]).astype(BF16)
    low[y, RANK : 2 * RANK, :] = dot_nt(wide_b, cot[...]).astype(BF16)
    for d in range(1, NY):
        send(low.at[y], low.at[y], ("low", d), at(y_=ys[d]))
    arrived(q2.at[y, 1 - zh, x, c], ("p2b", 0))
    for d in range(1, NX):
        send(q2.at[y, :, x, c], q2.at[y, :, x, c], ("p3b", d), at(x_=xs[d]))
    for d in range(1, NX):
        send(q1.at[zh, x, c], q1.at[zh, x, c], ("p3a", d), at(x_=xs[d]))
    drain("gax", "gaz", "gac", "gbz", "gbx", "gbc", "p1a", "p1b")
    for d in range(1, NY):
        arrived(low.at[from_y[d]], ("low", d))
    total = low[0].astype(F32)
    for yy in range(1, NY):
        total = total + low[yy].astype(F32)
    kept = (total * keep_ref[0].astype(F32)).astype(BF16)
    input_kept, grad_kept = kept[0:RANK], kept[RANK : 2 * RANK]

    chunk = 4
    for first in range(0, ROWS_A, chunk):
        part = dot_nn(grad_kept, act[:, first * LANES : (first + chunk) * LANES])
        for j in range(chunk):
            sa[:, first + j, :] = part[:, j * LANES : (j + 1) * LANES]
    mine, theirs = pl.ds(c * 32, 32), pl.ds(other * 32, 32)
    pa[...] = sa[theirs].reshape(NX, NZ, ROWS_A, LANES).astype(BF16)
    send(pa, r1a, ("c1a", 0), sibling)
    for first in range(0, ROWS_B, chunk):
        part = dot_nn(input_kept, cot[:, first * LANES : (first + chunk) * LANES])
        for j in range(chunk):
            sb[:, first + j, :] = part[:, j * LANES : (j + 1) * LANES]

    order = [1, 2, 3, 0]
    for d in order:
        rows = pl.ds(other * 32 + xs[d] * 8, 8)
        pb[d] = sb[rows].astype(BF16)
        send(pb.at[d], r1b.at[d], ("c1b", d), sibling)
    arrived(r1a, ("c1a", 0))
    for d in range(1, NX):
        arrived(q2.at[y, :, from_x[d], c], ("p3b", d))
    for d in range(1, NY):
        send(q2.at[y, :, :, c], q2.at[y, :, :, c], ("p4b", d), at(y_=ys[d]))
    pair_a = sa[mine].reshape(NX, NZ, ROWS_A, LANES) + r1a[...].astype(F32)
    f2a[...] = pair_a
    s2a[...] = pair_a.astype(BF16)
    for d in range(1, NZ):
        send(s2a.at[:, zs[d]], r2a.at[d], ("c2a", d), at(z_=zs[d]))
    for d in order:
        arrived(r1b.at[d], ("c1b", d))
        rows = pl.ds(c * 32 + xs[d] * 8, 8)
        pair = sb[rows] + r1b[d].astype(F32)
        if d:
            s2b[d] = pair.astype(BF16)
            send(s2b.at[d], r2b.at[d], ("c2b", d), at(x_=xs[d]))
        else:
            t32b[...] = pair
    drain("low", "c1a", "c1b", "p2b", "p3b")
    for d in range(1, NX):
        arrived(r2b.at[d], ("c2b", d))
    column = t32b[...]
    for d in range(1, NX):
        column = column + r2b[d].astype(F32)
    t32b[...] = column
    t16b[...] = column.astype(BF16)
    for d in range(1, NZ):
        send(t16b.at[zs[d]], r3b.at[d], ("c3b", d), at(z_=zs[d]))
    for d in range(1, NZ):
        arrived(r2a.at[d], ("c2a", d))
    line = f2a[:, z]
    for d in range(1, NZ):
        line = line + r2a[d].astype(F32)
    t32a[...] = line
    t16a[...] = line.astype(BF16)
    for d in range(1, NX):
        send(t16a.at[xs[d]], r3a.at[d], ("c3a", d), at(x_=xs[d]))
    arrived(q1.at[1 - zh, x, c], ("p2a", 0))
    for d in range(1, NX):
        send(q1.at[1 - zh, x, c], q1.at[1 - zh, x, c], ("p3c", d), at(x_=xs[d]))
    send(q2.at[y, :, :, c], q2.at[y, :, :, c], ("p5b", 0), sibling)
    send(q1.at[:, x, c], q1.at[:, x, c], ("p5a", 0), sibling)
    for d in range(1, NX):
        arrived(q1.at[zh, from_x[d], c], ("p3a", d))
    scale = adapter_scale / ROLLOUT_TOKENS
    for d in range(1, NX):
        arrived(r3a.at[d], ("c3a", d))
    grad_a = t32a[x]
    for d in range(1, NX):
        grad_a = grad_a + r3a[d].astype(F32)
    grad_a = grad_a * scale
    new_a, _, _ = adam_update(fa[:, 0, :], ma[:, 0, :], va[:, 0, :], grad_a)
    for h in range(2):
        ez[h, z] = new_a[8 * h : 8 * h + 8].astype(BF16)
    for d in range(1, NZ):
        send(ez.at[:, z], ez.at[:, z], ("ez", d), at(z_=zs[d]))
    for d in range(1, NZ):
        arrived(r3b.at[d], ("c3b", d))
    grad_b = t32b[z]
    for d in range(1, NZ):
        grad_b = grad_b + r3b[d].astype(F32)
    grad_b = grad_b * scale
    grad_out[0:ROWS_A] = grad_a
    grad_out[ROWS_A:ROWS] = grad_b
    new_b, _, _ = adam_update(fb[:, 0, :], mb[:, 0, :], vb[:, 0, :], grad_b)
    blocks = jnp.concatenate(in_wide_blocks(new_b), axis=0).astype(BF16)
    for kk in range(4):
        ebz[z, kk] = blocks[8 * kk : 8 * kk + 8]
    y_zh, y_x = lax.div(y, 2), lax.rem(y, 2)
    on_way = zh == y_zh
    holder = zh * 2 + lax.div(x, 2)
    holds = y == holder

    def send_if(condition, src, dst, key, device):
        one = copy(src, dst, key, device)
        sent.append((key[0], condition, one))
        pl.when(condition)(one.start)

    def arrived_if(condition, dst, key):
        pl.when(condition)(lambda: arrived(dst, key))

    for d in range(1, NZ):
        send_if(lax.div(zs[d], 4) == y_zh, ebz.at[z], ebz.at[z], ("bz", d), at(z_=zs[d]))

    for d in range(1, NY):
        arrived(q2.at[from_y[d], :, :, c], ("p4b", d))
        send(q2.at[from_y[d], :, :, c], q2.at[from_y[d], :, :, c], ("p5b", d), sibling)
    drain("c2a", "c2b", "c3a", "c3b", "p2a", "p3a", "p4b")
    for d in range(1, NZ):
        arrived(ez.at[:, from_z[d]], ("ez", d))
    for d in range(1, NX):
        send(ez.at[0], ea0.at[x], ("ex", d), at(x_=xs[d]))
    for d in range(1, NY):
        send(ez.at[1], ea1.at[y], ("ey", d), at(y_=ys[d]))
    ea0[x] = ez[0]
    ea1[y] = ez[1]
    for d in range(1, NZ):
        arrived_if(on_way, ebz.at[from_z[d]], ("bz", d))

    def two_blocks(xx):
        return ebz.at[:, pl.ds(lax.rem(xx, 2) * 2, 2)]

    for d in range(1, NX):
        target = jnp.logical_and(on_way, lax.div(xs[d], 2) == y_x)
        send_if(target, two_blocks(xs[d]), ebx.at[x], ("bx", d), at(x_=xs[d]))

    for d in range(1, NX):
        arrived(q1.at[1 - zh, from_x[d], c], ("p3c", d))
        send(q1.at[:, from_x[d], c], q1.at[:, from_x[d], c], ("p5a", d), sibling)
    load_base.wait()
    for d in range(NY):
        arrived(q2.at[from_y[d], :, :, other], ("p5b", d))
    total = jnp.zeros((BLOCK, 256), F32)
    for yy in range(NY):
        columns = slice(HALF + yy * PART, HALF + (yy + 1) * PART)
        total = total + dot_nt(base[:, columns], q2[yy].reshape(256, PART))
    part_out[...] = total

    for d in range(1, NX):
        arrived(ea0.at[from_x[d]], ("ex", d))
    for xx in range(NX):
        stga[xx * NZ : (xx + 1) * NZ] = ea0[xx].astype(F32)
    for j in range(8):
        ha0[y, c, :, j * LANES : (j + 1) * LANES] = stga[:, j, :].astype(BF16)
    for d in range(1, NY):
        send(ha0.at[y, c], ha0.at[y, c], ("fy", d), at(y_=ys[d]))
    send(ha0.at[y, c], ha0.at[y, c], ("fc", 0), sibling)
    for d in range(1, NY):
        arrived(ea1.at[from_y[d]], ("ey", d))
    for yy in range(NY):
        stgy[yy] = ea1[yy].astype(F32)
    for yy in range(NY):
        for j in range(8):
            ha1[yy, c, x, :, j * LANES : (j + 1) * LANES] = stgy[yy, :, j, :].astype(BF16)
    for d in range(1, NX):
        send(ha1.at[:, c, x], ha1.at[:, c, x], ("fx", d), at(x_=xs[d]))
    send(ha1.at[:, c, x], ha1.at[:, c, x], ("fd", 0), sibling)

    @pl.when(holds)
    def _():
        ebx[x] = ebz[:, pl.ds(lax.rem(x, 2) * 2, 2)]
        for d in range(1, NX):
            arrived(ebx.at[from_x[d]], ("bx", d))

    send_if(holds, ebx.at[:, :, other], ebd, ("bc", 0), sibling)

    for d in range(NX):
        arrived(q1.at[:, from_x[d], other], ("p5a", d))
    part_out[...] = part_out[...] + dot_nt(base[:, 0:HALF], q1[...].reshape(256, HALF))
    @pl.when(holds)
    def _():
        for xx in range(NX):
            stgb[c, xx * NZ : (xx + 1) * NZ] = ebx[xx, :, c].astype(F32)
        arrived(ebd, ("bc", 0))
        for xx in range(NX):
            stgb[other, xx * NZ : (xx + 1) * NZ] = ebd[xx].astype(F32)
        for yy in range(NY):
            for cc in range(NC):
                for h in range(2):
                    bs[yy, cc, :, h * LANES : (h + 1) * LANES] = stgb[
                        cc, :, 2 * yy + h, :
                    ].astype(BF16)
        bb[...] = bs[y]

    for d in range(1, NY):
        send_if(holds, bs.at[ys[d]], bb, ("by", d), at(y_=ys[d]))

    drain("ez", "ex", "ey", "p3c", "p5a", "p5b", "bz", "bx")
    for d in range(1, NY):
        arrived(ha0.at[from_y[d], c], ("fy", d))
        send(ha0.at[from_y[d], c], ha0.at[from_y[d], c], ("fc", d), sibling)
    for d in range(1, NX):
        arrived(ha1.at[:, c, from_x[d]], ("fx", d))
        send(ha1.at[:, c, from_x[d]], ha1.at[:, c, from_x[d]], ("fd", d), sibling)
    for d in range(NY):
        arrived(ha0.at[from_y[d], other], ("fc", d))
    for d in range(NX):
        arrived(ha1.at[:, other, from_x[d]], ("fd", d))

    cross = jnp.zeros((RANK, 256), F32)
    for yy in range(NY):
        left = (
            ha0[yy].reshape(RANK, PART),
            ha1[yy].astype(F32).reshape(RANK, PART).astype(BF16),
        )
        for h in range(2):
            if yy < 2:
                first = (2 * yy + h) * PART
                right = q1[:, :, :, :, first : first + PART].reshape(256, PART)
            else:
                right = q2[2 * (yy - 2) + h].reshape(256, PART)
            cross = cross + dot_nt(left[h], right)
    high = cross.astype(BF16)
    low_part = (cross - high.astype(F32)).astype(BF16)

    for d in range(1, NY):
        arrived_if(from_y[d] == holder, bb, ("by", d))
    turned = bb[...].reshape(RANK, WIDE).astype(F32).T.astype(BF16)[0:BLOCK]
    adapter = dot_nn(turned, high) + dot_nn(turned, low_part)
    part_out[...] = part_out[...] + adapter_scale * adapter

    drain()


SEMAPHORES = 128


def in_hbm(array):
    return pltpu.with_memory_space_constraint(array, pltpu.HBM)


def exchange(act, cot, keep, fa, ma, va, fb, mb, vb, prompts, base):
    hbm = pl.BlockSpec(memory_space=pltpu.HBM)
    vmem = pl.BlockSpec(memory_space=pltpu.VMEM)
    smem = pl.BlockSpec(memory_space=pltpu.SMEM)
    tokens = act.shape[0]
    sds = jax.ShapeDtypeStruct
    tile_a, tile_b = (ROWS_A, LANES), (ROWS_B, LANES)
    return pl.pallas_call(
        exchange_kernel,
        out_shape=(
            sds((ROWS, LANES), F32),
            sds((NY, NC, 32, 1024), BF16),
            sds((NY, NC, NX, 8, 1024), BF16),
            sds((NC, 32, WIDE), BF16),
            sds((BLOCK, 256), F32),
        ),
        in_specs=[hbm, hbm, smem] + [hbm] * 8,
        out_specs=(vmem,) * 5,
        scratch_shapes=[
            pltpu.VMEM((2, NX, NC, 16, 4096), BF16),
            pltpu.VMEM((NY, 2, NX, NC, 16, 1024), BF16),
            pltpu.VMEM(base.shape, BF16),
            pltpu.VMEM(act.shape, BF16),
            pltpu.VMEM(cot.shape, BF16),
            pltpu.VMEM(fa.shape, F32),
            pltpu.VMEM(fa.shape, F32),
            pltpu.VMEM(fa.shape, F32),
            pltpu.VMEM(fb.shape, F32),
            pltpu.VMEM(fb.shape, F32),
            pltpu.VMEM(fb.shape, F32),
            pltpu.VMEM((NC, NX, NZ, *tile_a), BF16),
            pltpu.VMEM((NC, NX, NZ, *tile_b), BF16),
            pltpu.VMEM((32, *tile_a), F32),
            pltpu.VMEM((NZ, *tile_b), F32),
            pltpu.VMEM((NC, 32, ROWS_A * LANES), F32),
            pltpu.VMEM((NC * NX, NZ, ROWS_B * LANES), F32),
            pltpu.VMEM((NY, 2 * RANK, tokens), BF16),
            pltpu.VMEM((RANK, *tile_a), F32),
            pltpu.VMEM((RANK, *tile_b), F32),
            pltpu.VMEM((NX, NZ, *tile_a), BF16),
            pltpu.VMEM((NX, NZ, *tile_b), BF16),
            pltpu.VMEM((NX, NZ, *tile_a), BF16),
            pltpu.VMEM((NX, NZ, *tile_b), BF16),
            pltpu.VMEM((NX, NZ, *tile_a), F32),
            pltpu.VMEM((NX, NZ, *tile_a), BF16),
            pltpu.VMEM((NX, NZ, *tile_b), BF16),
            pltpu.VMEM((NZ, NX, *tile_a), BF16),
            pltpu.VMEM((NX, NZ, *tile_b), BF16),
            pltpu.VMEM((NX, *tile_a), F32),
            pltpu.VMEM((NZ, *tile_b), F32),
            pltpu.VMEM((NX, *tile_a), BF16),
            pltpu.VMEM((NZ, *tile_b), BF16),
            pltpu.VMEM((NX, *tile_a), BF16),
            pltpu.VMEM((NZ, *tile_b), BF16),
            pltpu.VMEM((2, NZ, 8, LANES), BF16),
            pltpu.VMEM((NX, NZ, 8, LANES), BF16),
            pltpu.VMEM((NY, NZ, 8, LANES), BF16),
            pltpu.VMEM((NX * NZ, 8, LANES), F32),
            pltpu.VMEM((NY, NZ, 8, LANES), F32),
            pltpu.VMEM((NZ, 4, 8, LANES), BF16),
            pltpu.VMEM((NX, NZ, 2, 8, LANES), BF16),
            pltpu.VMEM((NX, NZ, 8, LANES), BF16),
            pltpu.VMEM((NC, NX * NZ, 8, LANES), F32),
            pltpu.VMEM((NY, NC, 32, WIDE), BF16),
            pltpu.VMEM((NY, 4, 4096), BF16),
            pltpu.VMEM((NY, 4, 1024), BF16),
            pltpu.VMEM((16, 4096), F32),
            pltpu.VMEM((16, 1024), F32),
            pltpu.SemaphoreType.DMA((11,)),
            pltpu.SemaphoreType.DMA((SEMAPHORES,)),
            pltpu.SemaphoreType.DMA((SEMAPHORES,)),
        ],
        compiler_params=pltpu.CompilerParams(
            collective_id=0, has_side_effects=True, vmem_limit_bytes=40 * 1024 * 1024
        ),
        cost_estimate=pl.CostEstimate(
            flops=200_000_000_000, bytes_accessed=8_000_000, transcendentals=0
        ),
        name="exchange",
    )(
        in_hbm(act),
        in_hbm(cot),
        keep,
        *map(in_hbm, (fa, ma, va, fb, mb, vb)),
        in_hbm(prompts),
        in_hbm(base),
    )


def merge_kernel(
    base, ha0, ha1, bb, part, grad, fa, ma, va, fb, mb, vb, ua, ub, na, nb, sa, sb, merged, proj, bt
):
    i = pl.program_id(0)

    @pl.when(i == 0)
    def _():
        bt[...] = bb[...].reshape(RANK, WIDE).astype(F32).T.astype(BF16)
        ua[:, 0, :], na[:, 0, :], sa[:, 0, :] = adam_update(
            fa[:, 0, :], ma[:, 0, :], va[:, 0, :], grad[0:ROWS_A]
        )
        ub[:, 0, :], nb[:, 0, :], sb[:, 0, :] = adam_update(
            fb[:, 0, :], mb[:, 0, :], vb[:, 0, :], grad[ROWS_A:ROWS]
        )
        proj[...] = part[...].astype(BF16)

    turned = bt[0:BLOCK, :]
    left = ha0[0].reshape(RANK, 1024)
    right = ha1[0].astype(F32).reshape(RANK, 1024).astype(BF16)
    for h, columns in enumerate((left, right)):
        here = slice(h * 1024, (h + 1) * 1024)
        delta = dot_nn(turned, columns)
        merged[:, here] = (base[:, here].astype(F32) + adapter_scale * delta).astype(BF16)


def merge(base, ha0, ha1, bb, part, grad, fa, ma, va, fb, mb, vb):
    sds = jax.ShapeDtypeStruct

    def fixed(shape):
        return pl.BlockSpec(shape, lambda i: (0,) * len(shape))

    a_shape, b_shape = (ROWS_A, 1, LANES), (ROWS_B, 1, LANES)
    return pl.pallas_call(
        merge_kernel,
        grid=(NY,),
        out_shape=(
            sds(a_shape, F32),
            sds(b_shape, F32),
            sds(a_shape, F32),
            sds(b_shape, F32),
            sds(a_shape, F32),
            sds(b_shape, F32),
            sds(base.shape, BF16),
            sds((BLOCK, 256), BF16),
        ),
        in_specs=[
            pl.BlockSpec((BLOCK, 2048), lambda i: (0, i)),
            pl.BlockSpec((1, NC, 32, 1024), lambda i: (i, 0, 0, 0)),
            pl.BlockSpec((1, NC, NX, 8, 1024), lambda i: (i, 0, 0, 0, 0)),
            fixed((NC, 32, WIDE)),
            fixed((BLOCK, 256)),
            fixed((ROWS, LANES)),
        ]
        + [fixed(a_shape)] * 3
        + [fixed(b_shape)] * 3,
        out_specs=[
            fixed(a_shape),
            fixed(b_shape),
            fixed(a_shape),
            fixed(b_shape),
            fixed(a_shape),
            fixed(b_shape),
            pl.BlockSpec((BLOCK, 2048), lambda i: (0, i)),
            fixed((BLOCK, 256)),
        ],
        scratch_shapes=[pltpu.VMEM((WIDE, RANK), BF16)],
        compiler_params=pltpu.CompilerParams(
            dimension_semantics=("arbitrary",), vmem_limit_bytes=16 * 1024 * 1024
        ),
        name="merge",
    )(base, ha0, ha1, bb, part, grad, fa, ma, va, fb, mb, vb)


def body(
    activations,
    cotangent,
    block_keep,
    input_factor,
    input_mean,
    input_square,
    output_factor,
    output_mean,
    output_square,
    frozen_base_rows,
    prompts,
):
    fa, ma, va = (v.reshape(ROWS_A, 1, LANES) for v in (input_factor, input_mean, input_square))
    fb, mb, vb = (v.reshape(ROWS_B, 1, LANES) for v in (output_factor, output_mean, output_square))
    grad, ha0, ha1, bb, part = exchange(
        activations,
        cotangent,
        block_keep,
        fa,
        ma,
        va,
        fb,
        mb,
        vb,
        prompts,
        frozen_base_rows,
    )
    ua, ub, na, nb, sa, sb, merged, projected = merge(
        frozen_base_rows, ha0, ha1, bb, part, grad, fa, ma, va, fb, mb, vb
    )
    return (
        ua.reshape(1, -1),
        ub.reshape(1, -1),
        na.reshape(1, -1),
        nb.reshape(1, -1),
        sa.reshape(1, -1),
        sb.reshape(1, -1),
        merged,
        projected,
    )


def solution(mesh):
    row = P(("role", "dp"), "tp")
    placed = (
        row,
        row,
        P(("role", "dp")),
        row,
        row,
        row,
        row,
        row,
        row,
        P(("dp", "tp"), None),
        P(("role", "dp", "tp"), None),
    )
    return jax.shard_map(
        body,
        mesh=mesh,
        in_specs=placed,
        out_specs=(
            row,
            row,
            row,
            row,
            row,
            row,
            P(("dp", "tp"), None),
            P(("dp", "tp"), "role"),
        ),
        check_vma=False,
    )
```

time: 70.5 us -> 66.4 us (0.942)
  Pallas kernels: 69 us -> 64.9 us
    pallas_call x1, Pallas kernels: 64.3 us -> 61.5 us  [exchange(): pl.pallas_call(exchange_kernel, out_shape=(sds((ROWS, LANES), F32), sds((...]
    pallas_call x1, Pallas kernels: 4.69 us -> 3.38 us  [merge(): pl.pallas_call(merge_kernel, grid=(NY,), out_shape=(sds(a_shape, F32), sd...]
where the time goes in v3:
time: 66.4 us; the launch traced here: 66.3 us
  Pallas kernels  64.9 us (98%)
  between operations  1.4 us (2%)
    pallas_call x1, Pallas kernels, exchange(): pl.pallas_call(exchange_kernel, out_shape=(sds((ROWS, LANES), F32), sds((...  61.5 us
    pallas_call x1, Pallas kernels, merge(): pl.pallas_call(merge_kernel, grid=(NY,), out_shape=(sds(a_shape, F32), sd...  3.38 us

profile of v3, /device:TPU:1, one launch (start us, length us, event | category | flops | bytes accessed | tf_op | source)
XLA Modules:
  0.0 66.3 jit_solution(6095823927114116577)
XLA Ops:
  1.3 0.0 copy-start
  1.3 0.0 copy-start.1
  1.3 0.0 copy-start.2
  1.3 0.0 copy-start.3
  1.3 0.0 copy-start.4
  1.3 0.0 copy-start.5
  1.3 0.0 copy-start.6
  1.4 61.5 %exchange.1 = (f32[44,128]{1,0:T(8,128)S(1)}, bf16[4,2,32,1024]{3,2,1,0:T(8,128)(2,1)S(1)}, bf16[4,2,4,8,1024]{4,3,2,1,0:T(8,128)(2,1)S(1)}, bf16[2,32,256]{2,1,0:T(8,128)(2,1)S(1)}, f32[224,256]{1,0:T(8,128)S(1)}) custom-call(bf16[256,2048]{1,0:T(8,128)(2,1)} %act_hbm.1, bf16[256,3584]{1,0:T(8,128)(2,1)} %cot_hbm.1, s32[1]{0:T(128)S(6)} %copy.19.keep_ref, ...), custom_call_target="tpu_custom_call" | custom-call | flops 199999995904 | bytes 8000000 | tf_op jit(solution)/shard_map/exchange/pallas_call | solution.py:558
  62.8 0.0 copy-done
  62.8 0.0 copy-done.1
  62.9 0.0 copy-done.2
  62.9 0.0 copy-done.3
  62.9 0.0 copy-done.4
  62.9 0.0 copy-done.5
  62.9 0.0 copy-done.6
  62.9 3.4 %merge.1 = (f32[16,1,128]{2,1,0:T(1,128)}, f32[28,1,128]{2,1,0:T(1,128)}, f32[16,1,128]{2,1,0:T(1,128)}, f32[28,1,128]{2,1,0:T(1,128)}, f32[16,1,128]{2,1,0:T(1,...) custom-call(bf16[224,8192]{1,0:T(8,128)(2,1)S(1)} %copy-done, ...), custom_call_target="tpu_custom_call" | custom-call | tf_op jit(solution)/shard_map/merge/pallas_call | solution.py:672
Async XLA Ops:
  1.3 61.6 %copy-start = (bf16[224,8192]{1,0:T(8,128)(2,1)S(1)}, bf16[224,8192]{1,0:T(8,128)(2,1)}, u32[]{:S(2)}) copy-start(bf16[224,8192]{1,0:T(8,128)(2,1)} %base.1) | copy-start | bytes 11010052
  1.3 61.6 %copy-start.1 = (f32[1,3584]{1,0:T(1,128)S(1)}, f32[1,3584]{1,0:T(1,128)}, u32[]{:S(2)}) copy-start(f32[1,3584]{1,0:T(1,128)} %param.17) | copy-start | bytes 43012
  1.3 61.6 %copy-start.2 = (f32[1,3584]{1,0:T(1,128)S(1)}, f32[1,3584]{1,0:T(1,128)}, u32[]{:S(2)}) copy-start(f32[1,3584]{1,0:T(1,128)} %param.18) | copy-start | bytes 43012
  1.3 61.6 %copy-start.3 = (f32[1,3584]{1,0:T(1,128)S(1)}, f32[1,3584]{1,0:T(1,128)}, u32[]{:S(2)}) copy-start(f32[1,3584]{1,0:T(1,128)} %param.19) | copy-start | bytes 43012
  1.3 61.6 %copy-start.4 = (f32[1,2048]{1,0:T(1,128)S(1)}, f32[1,2048]{1,0:T(1,128)}, u32[]{:S(2)}) copy-start(f32[1,2048]{1,0:T(1,128)} %param.14) | copy-start | bytes 24580
  1.3 61.6 %copy-start.5 = (f32[1,2048]{1,0:T(1,128)S(1)}, f32[1,2048]{1,0:T(1,128)}, u32[]{:S(2)}) copy-start(f32[1,2048]{1,0:T(1,128)} %param.15) | copy-start | bytes 24580
  1.3 61.6 %copy-start.6 = (f32[1,2048]{1,0:T(1,128)S(1)}, f32[1,2048]{1,0:T(1,128)}, u32[]{:S(2)}) copy-start(f32[1,2048]{1,0:T(1,128)} %param.16) | copy-start | bytes 24580

commit v4 on v3

v4 whole, which is shorter than its diff:
```python
import jax
import jax.numpy as jnp
from jax import lax
from jax.experimental import pallas as pl
from jax.experimental.pallas import tpu as pltpu
from jax.sharding import PartitionSpec as P

ROLLOUT_TOKENS = 256
RANK = 64
LANES = 128
ROWS_A, ROWS_B = 16, 28
ROWS = ROWS_A + ROWS_B
NX, NY, NZ, NC = 4, 4, 8, 2
BLOCK = 224
WIDE = 256
HALF, PART = 4096, 1024

adapter_scale = 2.0
learn_rate = 0.004
beta_one = 0.9
beta_two = 0.95
epsilon = 1e-08
first_fix = 1.0 - 0.9**20
second_fix = 1.0 - 0.95**20

F32, BF16 = jnp.float32, jnp.bfloat16
MESH = pl.DeviceIdType.MESH


def adam_update(factor, moment, square, gradient):
    moment_new = beta_one * moment + (1.0 - beta_one) * gradient
    square_new = beta_two * square + (1.0 - beta_two) * gradient * gradient
    factor_new = factor - learn_rate * (moment_new / first_fix) / (
        jnp.sqrt(square_new / second_fix) + epsilon
    )
    return (factor_new, moment_new, square_new)


def dot_nn(a, b):
    return lax.dot_general(a, b, (((1,), (0,)), ((), ())), preferred_element_type=F32)


def dot_nt(a, b):
    return lax.dot_general(a, b, (((1,), (1,)), ((), ())), preferred_element_type=F32)


def in_wide_blocks(rows):
    lane = lax.broadcasted_iota(jnp.int32, (1, LANES), 1)
    rolled = {0: rows}
    for off in (32, 64, 96):
        rolled[off] = pltpu.roll(rows, LANES - off, 1)
    out = []
    for k in range(16):
        row, off = divmod(BLOCK * k, LANES)
        turned = rolled[off]
        for half in range(2):
            first = turned[row + half : row + half + 1]
            if off == 0:
                out.append(first)
                continue
            last = min(row + half + 1, ROWS_B - 1)
            second = turned[last : last + 1]
            out.append(jnp.where(lane < LANES - off, first, second))
    return out


def exchange_kernel(
    act_hbm,
    cot_hbm,
    keep_ref,
    fa_hbm,
    ma_hbm,
    va_hbm,
    fb_hbm,
    mb_hbm,
    vb_hbm,
    prompts_hbm,
    base_hbm,
    grad_out,
    ha0,
    ha1,
    bb,
    part_out,
    cross_out,
    q1,
    q2,
    base,
    act,
    cot,
    fa,
    ma,
    va,
    fb,
    mb,
    vb,
    ga,
    gb,
    stg32,
    stg8,
    wa,
    wb,
    low,
    sa,
    sb,
    pa,
    pb,
    r1a,
    r1b,
    f2a,
    s2a,
    s2b,
    r2a,
    r2b,
    t32a,
    t32b,
    t16a,
    t16b,
    r3a,
    r3b,
    ez,
    ea0,
    ea1,
    stga,
    stgy,
    ebz,
    ebx,
    ebd,
    stgb,
    bs,
    pr1,
    pr2,
    pf1,
    pf2,
    loc,
    ssem,
    rsem,
):
    z_lo = lax.axis_index("role")
    dp = lax.axis_index("dp")
    y = lax.axis_index("tp")
    c = lax.rem(dp, 2)
    x = lax.rem(lax.div(dp, 2), 4)
    zh = lax.div(dp, 8)
    z = zh * 4 + z_lo

    def at(x_=x, y_=y, z_=z, c_=c):
        return {
            "role": lax.rem(z_, 4),
            "dp": lax.div(z_, 4) * 8 + x_ * 2 + c_,
            "tp": y_,
        }

    def step(v, d, n):
        return lax.rem(v + d, n)

    other = 1 - c
    sibling = at(c_=other)
    xs = [step(x, d, NX) for d in range(NX)]
    ys = [step(y, d, NY) for d in range(NY)]
    zs = [step(z, d, NZ) for d in range(NZ)]
    from_x = [step(x, NX - d, NX) for d in range(NX)]
    from_y = [step(y, NY - d, NY) for d in range(NY)]
    from_z = [step(z, NZ - d, NZ) for d in range(NZ)]

    stages, free, leaving, whole = {}, list(range(SENDS))[::-1], {}, {}

    def copy(src, dst, stage, key, device):
        return pltpu.make_async_remote_copy(
            src_ref=src,
            dst_ref=dst,
            send_sem=ssem.at[leaving[key][0]],
            recv_sem=rsem.at[stages.setdefault(stage, len(stages))],
            device_id=device,
            device_id_type=MESH,
        )

    def send(src, dst, stage, device):
        if stage not in leaving:
            leaving[stage] = (free.pop(), None, None)
        copy(src, dst, stage, stage, device).start()

    def send_if(condition, src, dst, stage, d, device):
        index = free.pop()
        leaving[stage, d] = (index, None, None)
        one = copy(src, dst, stage, (stage, d), device)
        leaving[stage, d] = (index, condition, one)
        pl.when(condition)(one.start)

    def arrived(all_of_it, stage):
        whole[stage] = all_of_it
        semaphore = rsem.at[stages[stage]]
        pltpu.make_async_copy(all_of_it, all_of_it, semaphore).wait()

    def drain(*keys):
        for key in keys:
            index, condition, one = leaving.pop(key)
            if one is None:
                pltpu.make_async_copy(whole[key], whole[key], ssem.at[index]).wait()
            else:
                pl.when(condition)(one.wait_send)
            free.append(index)

    load_act = pltpu.make_async_copy(act_hbm, act, loc.at[0])
    load_cot = pltpu.make_async_copy(cot_hbm, cot, loc.at[1])
    loads = [
        pltpu.make_async_copy(src, dst, loc.at[3 + i])
        for i, (src, dst) in enumerate(
            ((fa_hbm, fa), (fb_hbm, fb), (ma_hbm, ma), (va_hbm, va), (mb_hbm, mb), (vb_hbm, vb))
        )
    ]
    for one in loads[:2]:
        one.start()

    def late(yy):
        return prompts_hbm.at[:, pl.ds(pl.multiple_of(HALF + yy * PART, PART), PART)]

    early = prompts_hbm.at[:, 0:HALF]
    load_early = pltpu.make_async_copy(early, pr1.at[y], loc.at[2])
    load_late = pltpu.make_async_copy(late(y), pr2.at[y], loc.at[9])
    load_base = pltpu.make_async_copy(base_hbm, base, loc.at[10])
    load_early.start()
    load_late.start()
    load_act.start()
    load_cot.start()
    for one in loads[2:]:
        one.start()
    load_base.start()

    barrier = pltpu.get_barrier_semaphore()
    peers = (
        [sibling]
        + [at(x_=v) for v in xs[1:]]
        + [at(y_=v) for v in ys[1:]]
        + [at(z_=v) for v in zs[1:]]
    )
    for peer in peers:
        pl.semaphore_signal(barrier, inc=1, device_id=peer, device_id_type=MESH)

    for one in loads[:2]:
        one.wait()
    ga[c, x, z] = fa[:, 0, :].astype(BF16)
    gb[c, x, z] = fb[:, 0, :].astype(BF16)
    pl.semaphore_wait(barrier, len(peers))

    for d in range(1, NX):
        send(ga.at[c, x, z], ga.at[c, x, z], "gax", at(x_=xs[d]))
    for d in range(1, NZ):
        send(gb.at[c, x, z], gb.at[c, x, z], "gbz", at(z_=zs[d]))
    for d in range(1, NY):
        send(late(ys[d]), pr2.at[y], "p1b", at(y_=ys[d]))
    for d in range(1, NY):
        send(early, pr1.at[y], "p1a", at(y_=ys[d]))
    arrived(ga.at[c, 0 : NX - 1, z], "gax")
    for d in range(1, NZ):
        send(ga.at[c, :, z], ga.at[c, :, z], "gaz", at(z_=zs[d]))
    arrived(gb.at[c, x, 0 : NZ - 1], "gbz")
    for d in range(1, NX):
        send(gb.at[c, x], gb.at[c, x], "gbx", at(x_=xs[d]))
    send(gb.at[c, x], gb.at[c, x], "gbc", sibling)

    def spread_a(core):
        stg32[...] = ga[core].reshape(32, ROWS_A, LANES).astype(F32)
        for j in range(ROWS_A):
            wa[core, :, j * LANES : (j + 1) * LANES] = stg32[:, j, :]

    def spread_b(core, xx):
        stg8[...] = gb[core, xx].astype(F32)
        for j in range(ROWS_B):
            wb[core * 4 + xx, :, j * LANES : (j + 1) * LANES] = stg8[:, j, :]

    spread_b(c, x)

    z_pair = at(z_=step(z, 4, NZ))
    load_late.wait()
    arrived(pr2.at[0 : NY - 1], "p1b")
    for yy in range(NY):
        pf2[4 * yy : 4 * yy + 4, :] = pr2[yy].astype(F32)
    q2[y, zh, x, c] = pf2[...].astype(BF16)
    load_early.wait()
    arrived(pr1.at[0 : NY - 1], "p1a")
    for yy in range(NY):
        pf1[4 * yy : 4 * yy + 4, :] = pr1[yy].astype(F32)
    q1[zh, x, c] = pf1[...].astype(BF16)

    arrived(ga.at[c, :, 0 : NZ - 1], "gaz")
    send(ga.at[c], ga.at[c], "gac", sibling)
    send(q2.at[y, zh, x, c], q2.at[y, zh, x, c], "p2b", z_pair)
    spread_a(c)
    arrived(gb.at[c, 0 : NX - 1], "gbx")
    for d in range(1, NX):
        send(gb.at[c, from_x[d]], gb.at[c, from_x[d]], "gbc", sibling)
        spread_b(c, from_x[d])
    for d in range(1, NX):
        send(q1.at[zh, x, c], q1.at[zh, x, c], "p3a", at(x_=xs[d]))
    arrived(ga.at[other], "gac")
    send(q1.at[zh, x, c], q1.at[zh, x, c], "p2a", z_pair)
    spread_a(other)
    arrived(gb.at[other], "gbc")
    for d in range(NX):
        spread_b(other, from_x[d])

    load_act.wait()
    load_cot.wait()
    for one in loads[2:]:
        one.wait()
    wide_a = wa[...].reshape(RANK, ROWS_A * LANES).astype(BF16)
    wide_b = wb[...].reshape(RANK, ROWS_B * LANES).astype(BF16)
    low[y, :, 0:RANK] = dot_nt(act[...], wide_a).astype(BF16)
    low[y, :, RANK : 2 * RANK] = dot_nt(cot[...], wide_b).astype(BF16)
    for d in range(1, NY):
        send(low.at[y], low.at[y], "low", at(y_=ys[d]))
    arrived(q2.at[y, 1 - zh, x, c], "p2b")
    for d in range(1, NX):
        send(q2.at[y, :, x, c], q2.at[y, :, x, c], "p3b", at(x_=xs[d]))
    drain("gax", "gaz", "gac", "gbz", "gbx", "gbc", "p1a", "p1b")
    arrived(low.at[0 : NY - 1], "low")
    total = low[0].astype(F32)
    for yy in range(1, NY):
        total = total + low[yy].astype(F32)
    kept = (total * keep_ref[0].astype(F32)).T.astype(BF16)
    input_kept, grad_kept = kept[0:RANK], kept[RANK : 2 * RANK]

    chunk = 4
    for first in range(0, ROWS_A, chunk):
        part = dot_nn(grad_kept, act[:, first * LANES : (first + chunk) * LANES])
        for j in range(chunk):
            sa[:, first + j, :] = part[:, j * LANES : (j + 1) * LANES]
    mine, theirs = pl.ds(c * 32, 32), pl.ds(other * 32, 32)
    pa[...] = sa[theirs].reshape(NX, NZ, ROWS_A, LANES).astype(BF16)
    send(pa, r1a, "c1a", sibling)
    for first in range(0, ROWS_B, chunk):
        part = dot_nn(input_kept, cot[:, first * LANES : (first + chunk) * LANES])
        for j in range(chunk):
            sb[:, first + j, :] = part[:, j * LANES : (j + 1) * LANES]

    order = [1, 2, 3, 0]
    for d in order:
        rows = pl.ds(other * 32 + xs[d] * 8, 8)
        pb[d] = sb[rows].astype(BF16)
        send(pb.at[d], r1b.at[d], f"c1b{d}", sibling)
    arrived(r1a, "c1a")
    pair_a = sa[mine].reshape(NX, NZ, ROWS_A, LANES) + r1a[...].astype(F32)
    f2a[...] = pair_a
    s2a[...] = pair_a.astype(BF16)
    for d in range(1, NZ):
        send(s2a.at[:, zs[d]], r2a.at[d], "c2a", at(z_=zs[d]))
    for d in order:
        arrived(r1b.at[d], f"c1b{d}")
        rows = pl.ds(c * 32 + xs[d] * 8, 8)
        pair = sb[rows] + r1b[d].astype(F32)
        if d:
            s2b[d] = pair.astype(BF16)
            send(s2b.at[d], r2b.at[d], "c2b", at(x_=xs[d]))
        else:
            t32b[...] = pair
    arrived(q2.at[y, :, 0 : NX - 1, c], "p3b")
    for d in range(1, NY):
        send(q2.at[y, :, :, c], q2.at[y, :, :, c], "p4b", at(y_=ys[d]))
    drain("low", "c1a", *(f"c1b{d}" for d in order), "p2b")
    arrived(r2b.at[1:NX], "c2b")
    column = t32b[...]
    for d in range(1, NX):
        column = column + r2b[d].astype(F32)
    t32b[...] = column
    t16b[...] = column.astype(BF16)
    for d in range(1, NZ):
        send(t16b.at[zs[d]], r3b.at[d], "c3b", at(z_=zs[d]))
    arrived(r2a.at[1:NZ], "c2a")
    line = f2a[:, z]
    for d in range(1, NZ):
        line = line + r2a[d].astype(F32)
    t32a[...] = line
    t16a[...] = line.astype(BF16)
    for d in range(1, NX):
        send(t16a.at[xs[d]], r3a.at[d], "c3a", at(x_=xs[d]))
    arrived(q1.at[1 - zh, x, c], "p2a")
    for d in range(1, NX):
        send(q1.at[1 - zh, x, c], q1.at[1 - zh, x, c], "p3c", at(x_=xs[d]))
    send(q2.at[y, :, :, c], q2.at[y, :, :, c], "p5b", sibling)
    send(q1.at[:, x, c], q1.at[:, x, c], "p5a", sibling)
    arrived(q1.at[0, 0 : NX - 1, c], "p3a")
    scale = adapter_scale / ROLLOUT_TOKENS
    arrived(r3a.at[1:NX], "c3a")
    grad_a = t32a[x]
    for d in range(1, NX):
        grad_a = grad_a + r3a[d].astype(F32)
    grad_a = grad_a * scale
    new_a, _, _ = adam_update(fa[:, 0, :], ma[:, 0, :], va[:, 0, :], grad_a)
    for h in range(2):
        ez[h, z] = new_a[8 * h : 8 * h + 8].astype(BF16)
    for d in range(1, NZ):
        send(ez.at[:, z], ez.at[:, z], "ez", at(z_=zs[d]))
    arrived(r3b.at[1:NZ], "c3b")
    grad_b = t32b[z]
    for d in range(1, NZ):
        grad_b = grad_b + r3b[d].astype(F32)
    grad_b = grad_b * scale
    grad_out[0:ROWS_A] = grad_a
    grad_out[ROWS_A:ROWS] = grad_b
    new_b, _, _ = adam_update(fb[:, 0, :], mb[:, 0, :], vb[:, 0, :], grad_b)
    blocks = jnp.concatenate(in_wide_blocks(new_b), axis=0).astype(BF16)
    for kk in range(4):
        ebz[z, kk] = blocks[8 * kk : 8 * kk + 8]
    y_zh, y_x = lax.div(y, 2), lax.rem(y, 2)
    on_way = zh == y_zh
    holder = zh * 2 + lax.div(x, 2)
    holds = y == holder

    def arrived_if(condition, dst, stage):
        pl.when(condition)(lambda: arrived(dst, stage))

    for d in range(1, NZ):
        send_if(lax.div(zs[d], 4) == y_zh, ebz.at[z], ebz.at[z], "bz", d, at(z_=zs[d]))

    drain("c2a", "c2b", "c3a", "c3b", "p2a", "p3a", "p3b")
    arrived(ez.at[:, 0 : NZ - 1], "ez")
    for d in range(1, NX):
        send(ez.at[0], ea0.at[x], "ex", at(x_=xs[d]))
    for d in range(1, NY):
        send(ez.at[1], ea1.at[y], "ey", at(y_=ys[d]))
    ea0[x] = ez[0]
    ea1[y] = ez[1]
    arrived_if(on_way, ebz.at[0 : NZ - 1], "bz")

    def two_blocks(xx):
        return ebz.at[:, pl.ds(lax.rem(xx, 2) * 2, 2)]

    for d in range(1, NX):
        target = jnp.logical_and(on_way, lax.div(xs[d], 2) == y_x)
        send_if(target, two_blocks(xs[d]), ebx.at[x], "bx", d, at(x_=xs[d]))

    arrived(q2.at[0 : NY - 1, :, :, c], "p4b")
    for d in range(1, NY):
        send(q2.at[from_y[d], :, :, c], q2.at[from_y[d], :, :, c], "p5b", sibling)
    arrived(q1.at[0, 0 : NX - 1, c], "p3c")
    for d in range(1, NX):
        send(q1.at[:, from_x[d], c], q1.at[:, from_x[d], c], "p5a", sibling)
    arrived(ea0.at[0 : NX - 1], "ex")
    for xx in range(NX):
        stga[xx * NZ : (xx + 1) * NZ] = ea0[xx].astype(F32)
    for j in range(8):
        ha0[y, c, :, j * LANES : (j + 1) * LANES] = stga[:, j, :].astype(BF16)
    for d in range(1, NY):
        send(ha0.at[y, c], ha0.at[y, c], "fy", at(y_=ys[d]))
    send(ha0.at[y, c], ha0.at[y, c], "fc", sibling)
    arrived(ea1.at[0 : NY - 1], "ey")
    for yy in range(NY):
        stgy[yy] = ea1[yy].astype(F32)
    for yy in range(NY):
        for j in range(8):
            ha1[yy, c, x, :, j * LANES : (j + 1) * LANES] = stgy[yy, :, j, :].astype(BF16)
    for d in range(1, NX):
        send(ha1.at[:, c, x], ha1.at[:, c, x], "fx", at(x_=xs[d]))
    send(ha1.at[:, c, x], ha1.at[:, c, x], "fd", sibling)

    @pl.when(holds)
    def _():
        ebx[x] = ebz[:, pl.ds(lax.rem(x, 2) * 2, 2)]
        arrived(ebx.at[0 : NX - 1], "bx")

    send_if(holds, ebx.at[:, :, other], ebd, "bc", 0, sibling)

    load_base.wait()
    arrived(q2.at[:, :, :, other], "p5b")
    total = jnp.zeros((BLOCK, 256), F32)
    for yy in range(NY):
        columns = slice(HALF + yy * PART, HALF + (yy + 1) * PART)
        total = total + dot_nt(base[:, columns], q2[yy].reshape(256, PART))
    part_out[...] = total

    @pl.when(holds)
    def _():
        for xx in range(NX):
            stgb[c, xx * NZ : (xx + 1) * NZ] = ebx[xx, :, c].astype(F32)
        arrived(ebd, "bc")
        for xx in range(NX):
            stgb[other, xx * NZ : (xx + 1) * NZ] = ebd[xx].astype(F32)
        for yy in range(NY):
            for cc in range(NC):
                for h in range(2):
                    bs[yy, cc, :, h * LANES : (h + 1) * LANES] = stgb[
                        cc, :, 2 * yy + h, :
                    ].astype(BF16)
        bb[...] = bs[y]

    for d in range(1, NY):
        send_if(holds, bs.at[ys[d]], bb, "by", d, at(y_=ys[d]))

    arrived(q1.at[:, :, other], "p5a")
    part_out[...] = part_out[...] + dot_nt(base[:, 0:HALF], q1[...].reshape(256, HALF))
    drain("ez", "ex", "ey", "p3c", "p4b", "p5a", "p5b", *((k, d) for k, n in (("bz", NZ), ("bx", NX)) for d in range(1, n)))
    arrived(ha0.at[0 : NY - 1, c], "fy")
    for d in range(1, NY):
        send(ha0.at[from_y[d], c], ha0.at[from_y[d], c], "fc", sibling)
    arrived(ha1.at[:, c, 0 : NX - 1], "fx")
    for d in range(1, NX):
        send(ha1.at[:, c, from_x[d]], ha1.at[:, c, from_x[d]], "fd", sibling)
    arrived(ha0.at[:, other], "fc")
    arrived(ha1.at[:, other], "fd")

    cross = jnp.zeros((256, RANK), F32)
    for yy in range(NY):
        left = (
            ha0[yy].reshape(RANK, PART),
            ha1[yy].astype(F32).reshape(RANK, PART).astype(BF16),
        )
        for h in range(2):
            if yy < 2:
                first = (2 * yy + h) * PART
                right = q1[:, :, :, :, first : first + PART].reshape(256, PART)
            else:
                right = q2[2 * (yy - 2) + h].reshape(256, PART)
            cross = cross + dot_nt(right, left[h])
    high = cross.astype(BF16)
    cross_out[:, 0:RANK] = high
    cross_out[:, RANK : 2 * RANK] = (cross - high.astype(F32)).astype(BF16)

    arrived_if(y != holder, bb, "by")
    drain(*leaving)


ARRIVALS, SENDS = 37, 26


def in_hbm(array):
    return pltpu.with_memory_space_constraint(array, pltpu.HBM)


def exchange(act, cot, keep, fa, ma, va, fb, mb, vb, prompts, base):
    hbm = pl.BlockSpec(memory_space=pltpu.HBM)
    vmem = pl.BlockSpec(memory_space=pltpu.VMEM)
    smem = pl.BlockSpec(memory_space=pltpu.SMEM)
    tokens = act.shape[0]
    sds = jax.ShapeDtypeStruct
    tile_a, tile_b = (ROWS_A, LANES), (ROWS_B, LANES)
    return pl.pallas_call(
        exchange_kernel,
        out_shape=(
            sds((ROWS, LANES), F32),
            sds((NY, NC, 32, 1024), BF16),
            sds((NY, NC, NX, 8, 1024), BF16),
            sds((NC, 32, WIDE), BF16),
            sds((BLOCK, 256), F32),
            sds((256, 2 * RANK), BF16),
        ),
        in_specs=[hbm, hbm, smem] + [hbm] * 8,
        out_specs=(vmem,) * 6,
        scratch_shapes=[
            pltpu.VMEM((2, NX, NC, 16, 4096), BF16),
            pltpu.VMEM((NY, 2, NX, NC, 16, 1024), BF16),
            pltpu.VMEM(base.shape, BF16),
            pltpu.VMEM(act.shape, BF16),
            pltpu.VMEM(cot.shape, BF16),
            pltpu.VMEM(fa.shape, F32),
            pltpu.VMEM(fa.shape, F32),
            pltpu.VMEM(fa.shape, F32),
            pltpu.VMEM(fb.shape, F32),
            pltpu.VMEM(fb.shape, F32),
            pltpu.VMEM(fb.shape, F32),
            pltpu.VMEM((NC, NX, NZ, *tile_a), BF16),
            pltpu.VMEM((NC, NX, NZ, *tile_b), BF16),
            pltpu.VMEM((32, *tile_a), F32),
            pltpu.VMEM((NZ, *tile_b), F32),
            pltpu.VMEM((NC, 32, ROWS_A * LANES), F32),
            pltpu.VMEM((NC * NX, NZ, ROWS_B * LANES), F32),
            pltpu.VMEM((NY, tokens, 2 * RANK), BF16),
            pltpu.VMEM((RANK, *tile_a), F32),
            pltpu.VMEM((RANK, *tile_b), F32),
            pltpu.VMEM((NX, NZ, *tile_a), BF16),
            pltpu.VMEM((NX, NZ, *tile_b), BF16),
            pltpu.VMEM((NX, NZ, *tile_a), BF16),
            pltpu.VMEM((NX, NZ, *tile_b), BF16),
            pltpu.VMEM((NX, NZ, *tile_a), F32),
            pltpu.VMEM((NX, NZ, *tile_a), BF16),
            pltpu.VMEM((NX, NZ, *tile_b), BF16),
            pltpu.VMEM((NZ, NX, *tile_a), BF16),
            pltpu.VMEM((NX, NZ, *tile_b), BF16),
            pltpu.VMEM((NX, *tile_a), F32),
            pltpu.VMEM((NZ, *tile_b), F32),
            pltpu.VMEM((NX, *tile_a), BF16),
            pltpu.VMEM((NZ, *tile_b), BF16),
            pltpu.VMEM((NX, *tile_a), BF16),
            pltpu.VMEM((NZ, *tile_b), BF16),
            pltpu.VMEM((2, NZ, 8, LANES), BF16),
            pltpu.VMEM((NX, NZ, 8, LANES), BF16),
            pltpu.VMEM((NY, NZ, 8, LANES), BF16),
            pltpu.VMEM((NX * NZ, 8, LANES), F32),
            pltpu.VMEM((NY, NZ, 8, LANES), F32),
            pltpu.VMEM((NZ, 4, 8, LANES), BF16),
            pltpu.VMEM((NX, NZ, 2, 8, LANES), BF16),
            pltpu.VMEM((NX, NZ, 8, LANES), BF16),
            pltpu.VMEM((NC, NX * NZ, 8, LANES), F32),
            pltpu.VMEM((NY, NC, 32, WIDE), BF16),
            pltpu.VMEM((NY, 4, 4096), BF16),
            pltpu.VMEM((NY, 4, 1024), BF16),
            pltpu.VMEM((16, 4096), F32),
            pltpu.VMEM((16, 1024), F32),
            pltpu.SemaphoreType.DMA((11,)),
            pltpu.SemaphoreType.DMA((SENDS,)),
            pltpu.SemaphoreType.DMA((ARRIVALS,)),
        ],
        compiler_params=pltpu.CompilerParams(
            collective_id=0, has_side_effects=True, vmem_limit_bytes=40 * 1024 * 1024
        ),
        cost_estimate=pl.CostEstimate(
            flops=200_000_000_000, bytes_accessed=8_000_000, transcendentals=0
        ),
        name="exchange",
    )(
        in_hbm(act),
        in_hbm(cot),
        keep,
        *map(in_hbm, (fa, ma, va, fb, mb, vb)),
        in_hbm(prompts),
        in_hbm(base),
    )


def merge_kernel(
    base,
    ha0,
    ha1,
    bb,
    part,
    cross,
    grad,
    fa,
    ma,
    va,
    fb,
    mb,
    vb,
    ua,
    ub,
    na,
    nb,
    sa,
    sb,
    merged,
    proj,
    rows,
    done,
):
    turned = bb[...].reshape(RANK, WIDE).astype(F32).T.astype(BF16)[0:BLOCK]
    copies = []
    for yy in range(NY):
        left = ha0[yy].reshape(RANK, PART)
        right = ha1[yy].astype(F32).reshape(RANK, PART).astype(BF16)
        for h, columns in enumerate((left, right)):
            first = (2 * yy + h) * PART
            here = slice(first, first + PART)
            delta = dot_nn(turned, columns)
            rows[:, here] = (base[:, here].astype(F32) + adapter_scale * delta).astype(BF16)
            one = pltpu.make_async_copy(rows.at[:, here], merged.at[:, here], done.at[2 * yy + h])
            one.start()
            copies.append(one)
    ua[:, 0, :], na[:, 0, :], sa[:, 0, :] = adam_update(
        fa[:, 0, :], ma[:, 0, :], va[:, 0, :], grad[0:ROWS_A]
    )
    ub[:, 0, :], nb[:, 0, :], sb[:, 0, :] = adam_update(
        fb[:, 0, :], mb[:, 0, :], vb[:, 0, :], grad[ROWS_A:ROWS]
    )
    twice = jnp.concatenate([turned, turned], axis=1)
    proj[...] = (part[...] + adapter_scale * dot_nt(twice, cross[...])).astype(BF16)
    for one in copies:
        one.wait()


def merge(base, ha0, ha1, bb, part, cross, grad, fa, ma, va, fb, mb, vb):
    sds = jax.ShapeDtypeStruct
    vmem = pl.BlockSpec(memory_space=pltpu.VMEM)
    a_shape, b_shape = (ROWS_A, 1, LANES), (ROWS_B, 1, LANES)
    return pl.pallas_call(
        merge_kernel,
        out_shape=(
            sds(a_shape, F32),
            sds(b_shape, F32),
            sds(a_shape, F32),
            sds(b_shape, F32),
            sds(a_shape, F32),
            sds(b_shape, F32),
            sds(base.shape, BF16),
            sds((BLOCK, 256), BF16),
        ),
        in_specs=[vmem] * 13,
        out_specs=(vmem,) * 6 + (pl.BlockSpec(memory_space=pltpu.HBM), vmem),
        scratch_shapes=[pltpu.VMEM(base.shape, BF16), pltpu.SemaphoreType.DMA((2 * NY,))],
        compiler_params=pltpu.CompilerParams(vmem_limit_bytes=16 * 1024 * 1024),
        name="merge",
    )(base, ha0, ha1, bb, part, cross, grad, fa, ma, va, fb, mb, vb)


def body(
    activations,
    cotangent,
    block_keep,
    input_factor,
    input_mean,
    input_square,
    output_factor,
    output_mean,
    output_square,
    frozen_base_rows,
    prompts,
):
    fa, ma, va = (v.reshape(ROWS_A, 1, LANES) for v in (input_factor, input_mean, input_square))
    fb, mb, vb = (v.reshape(ROWS_B, 1, LANES) for v in (output_factor, output_mean, output_square))
    grad, ha0, ha1, bb, part, cross = exchange(
        activations,
        cotangent,
        block_keep,
        fa,
        ma,
        va,
        fb,
        mb,
        vb,
        prompts,
        frozen_base_rows,
    )
    ua, ub, na, nb, sa, sb, merged, projected = merge(
        frozen_base_rows, ha0, ha1, bb, part, cross, grad, fa, ma, va, fb, mb, vb
    )
    return (
        ua.reshape(1, -1),
        ub.reshape(1, -1),
        na.reshape(1, -1),
        nb.reshape(1, -1),
        sa.reshape(1, -1),
        sb.reshape(1, -1),
        merged,
        projected,
    )


def solution(mesh):
    row = P(("role", "dp"), "tp")
    placed = (
        row,
        row,
        P(("role", "dp")),
        row,
        row,
        row,
        row,
        row,
        row,
        P(("dp", "tp"), None),
        P(("role", "dp", "tp"), None),
    )
    return jax.shard_map(
        body,
        mesh=mesh,
        in_specs=placed,
        out_specs=(
            row,
            row,
            row,
            row,
            row,
            row,
            P(("dp", "tp"), None),
            P(("dp", "tp"), "role"),
        ),
        check_vma=False,
    )
```

time: 66.4 us -> 64.1 us (0.965)
  Pallas kernels: 64.9 us -> 62.6 us
    pallas_call x1, Pallas kernels: 61.5 us -> 59.5 us  [exchange(): pl.pallas_call(exchange_kernel, out_shape=(sds((ROWS, LANES), F32), sds((...]
where the time goes in v4:
time: 64.1 us
  Pallas kernels  62.6 us (98%)
  between operations  1.4 us (2%)
    pallas_call x1, Pallas kernels, exchange(): pl.pallas_call(exchange_kernel, out_shape=(sds((ROWS, LANES), F32), sds((...  59.5 us
    pallas_call x1, Pallas kernels, merge(): pl.pallas_call(merge_kernel, out_shape=(sds(a_shape, F32), sds(b_shape, F...  3.13 us

profile of v4, /device:TPU:1, one launch (start us, length us, event | category | flops | bytes accessed | tf_op | source)
XLA Modules:
  0.0 64.1 jit_solution(2529748453774815926)
XLA Ops:
  1.3 0.0 copy-start
  1.3 0.0 copy-start.1
  1.3 0.0 copy-start.2
  1.3 0.0 copy-start.3
  1.3 0.0 copy-start.4
  1.3 0.0 copy-start.5
  1.3 0.0 copy-start.6
  1.4 59.5 %exchange.1 = (f32[44,128]{1,0:T(8,128)S(1)}, bf16[4,2,32,1024]{3,2,1,0:T(8,128)(2,1)S(1)}, bf16[4,2,4,8,1024]{4,3,2,1,0:T(8,128)(2,1)S(1)}, bf16[2,32,256]{2,1,...) custom-call(bf16[256,2048]{1,0:T(8,128)(2,1)} %act_hbm.1, bf16[256,3584]{1,0:T(8,128)(2,1)} %cot_hbm.1, ...), custom_call_target="tpu_custom_call" | custom-call | flops 199999995904 | bytes 8000000 | tf_op jit(solution)/shard_map/exchange/pallas_call | solution.py:536
  60.9 0.0 copy-done
  60.9 0.0 copy-done.1
  60.9 0.0 copy-done.2
  60.9 0.0 copy-done.3
  60.9 0.0 copy-done.4
  60.9 0.0 copy-done.5
  60.9 0.0 copy-done.6
  60.9 3.1 %merge.1 = (f32[16,1,128]{2,1,0:T(1,128)}, f32[28,1,128]{2,1,0:T(1,128)}, f32[16,1,128]{2,1,0:T(1,128)}, f32[28,1,128]{2,1,0:T(1,128)}, f32[16,1,128]{2,1,0:T(1,...) custom-call(bf16[224,8192]{1,0:T(8,128)(2,1)S(1)} %copy-done, ...), custom_call_target="tpu_custom_call" | custom-call | tf_op jit(solution)/shard_map/merge/pallas_call | solution.py:673
Async XLA Ops:
  1.3 59.6 %copy-start = (bf16[224,8192]{1,0:T(8,128)(2,1)S(1)}, bf16[224,8192]{1,0:T(8,128)(2,1)}, u32[]{:S(2)}) copy-start(bf16[224,8192]{1,0:T(8,128)(2,1)} %base.1) | copy-start | bytes 11010052
  1.3 59.6 %copy-start.1 = (f32[1,3584]{1,0:T(1,128)S(1)}, f32[1,3584]{1,0:T(1,128)}, u32[]{:S(2)}) copy-start(f32[1,3584]{1,0:T(1,128)} %param.17) | copy-start | bytes 43012
  1.3 59.6 %copy-start.2 = (f32[1,3584]{1,0:T(1,128)S(1)}, f32[1,3584]{1,0:T(1,128)}, u32[]{:S(2)}) copy-start(f32[1,3584]{1,0:T(1,128)} %param.18) | copy-start | bytes 43012
  1.3 59.6 %copy-start.3 = (f32[1,3584]{1,0:T(1,128)S(1)}, f32[1,3584]{1,0:T(1,128)}, u32[]{:S(2)}) copy-start(f32[1,3584]{1,0:T(1,128)} %param.19) | copy-start | bytes 43012
  1.3 59.6 %copy-start.4 = (f32[1,2048]{1,0:T(1,128)S(1)}, f32[1,2048]{1,0:T(1,128)}, u32[]{:S(2)}) copy-start(f32[1,2048]{1,0:T(1,128)} %param.14) | copy-start | bytes 24580
  1.3 59.6 %copy-start.5 = (f32[1,2048]{1,0:T(1,128)S(1)}, f32[1,2048]{1,0:T(1,128)}, u32[]{:S(2)}) copy-start(f32[1,2048]{1,0:T(1,128)} %param.15) | copy-start | bytes 24580
  1.3 59.6 %copy-start.6 = (f32[1,2048]{1,0:T(1,128)S(1)}, f32[1,2048]{1,0:T(1,128)}, u32[]{:S(2)}) copy-start(f32[1,2048]{1,0:T(1,128)} %param.16) | copy-start | bytes 24580

commit v5 on v4

--- a/solution.py
+++ b/solution.py
@@ -81,7 +81,6 @@
     ha1,
     bb,
     part_out,
-    cross_out,
     q1,
     q2,
     base,
@@ -443,6 +442,13 @@
     for d in range(1, NY):
         send(ha0.at[y, c], ha0.at[y, c], "fy", at(y_=ys[d]))
     send(ha0.at[y, c], ha0.at[y, c], "fc", sibling)
+    @pl.when(holds)
+    def _():
+        ebx[x] = ebz[:, pl.ds(lax.rem(x, 2) * 2, 2)]
+        arrived(ebx.at[0 : NX - 1], "bx")
+
+    send_if(holds, ebx.at[:, :, other], ebd, "bc", 0, sibling)
+
     arrived(ea1.at[0 : NY - 1], "ey")
     for yy in range(NY):
         stgy[yy] = ea1[yy].astype(F32)
@@ -452,21 +458,6 @@
     for d in range(1, NX):
         send(ha1.at[:, c, x], ha1.at[:, c, x], "fx", at(x_=xs[d]))
     send(ha1.at[:, c, x], ha1.at[:, c, x], "fd", sibling)
-
-    @pl.when(holds)
-    def _():
-        ebx[x] = ebz[:, pl.ds(lax.rem(x, 2) * 2, 2)]
-        arrived(ebx.at[0 : NX - 1], "bx")
-
-    send_if(holds, ebx.at[:, :, other], ebd, "bc", 0, sibling)
-
-    load_base.wait()
-    arrived(q2.at[:, :, :, other], "p5b")
-    total = jnp.zeros((BLOCK, 256), F32)
-    for yy in range(NY):
-        columns = slice(HALF + yy * PART, HALF + (yy + 1) * PART)
-        total = total + dot_nt(base[:, columns], q2[yy].reshape(256, PART))
-    part_out[...] = total
 
     @pl.when(holds)
     def _():
@@ -486,9 +477,18 @@
     for d in range(1, NY):
         send_if(holds, bs.at[ys[d]], bb, "by", d, at(y_=ys[d]))
 
+    load_base.wait()
+    arrived(q2.at[:, :, :, other], "p5b")
+    total = jnp.zeros((BLOCK, 256), F32)
+    for yy in range(NY):
+        columns = slice(HALF + yy * PART, HALF + (yy + 1) * PART)
+        total = total + dot_nt(base[:, columns], q2[yy].reshape(256, PART))
+    part_out[...] = total
+
     arrived(q1.at[:, :, other], "p5a")
     part_out[...] = part_out[...] + dot_nt(base[:, 0:HALF], q1[...].reshape(256, HALF))
-    drain("ez", "ex", "ey", "p3c", "p4b", "p5a", "p5b", *((k, d) for k, n in (("bz", NZ), ("bx", NX)) for d in range(1, n)))
+    b_sends = [("bz", d) for d in range(1, NZ)] + [("bx", d) for d in range(1, NX)]
+    drain("ez", "ex", "ey", "p3c", "p4b", "p5a", "p5b", *b_sends)
     arrived(ha0.at[0 : NY - 1, c], "fy")
     for d in range(1, NY):
         send(ha0.at[from_y[d], c], ha0.at[from_y[d], c], "fc", sibling)
@@ -497,23 +497,6 @@
         send(ha1.at[:, c, from_x[d]], ha1.at[:, c, from_x[d]], "fd", sibling)
     arrived(ha0.at[:, other], "fc")
     arrived(ha1.at[:, other], "fd")
-
-    cross = jnp.zeros((256, RANK), F32)
-    for yy in range(NY):
-        left = (
-            ha0[yy].reshape(RANK, PART),
-            ha1[yy].astype(F32).reshape(RANK, PART).astype(BF16),
-        )
-        for h in range(2):
-            if yy < 2:
-                first = (2 * yy + h) * PART
-                right = q1[:, :, :, :, first : first + PART].reshape(256, PART)
-            else:
-                right = q2[2 * (yy - 2) + h].reshape(256, PART)
-            cross = cross + dot_nt(right, left[h])
-    high = cross.astype(BF16)
-    cross_out[:, 0:RANK] = high
-    cross_out[:, RANK : 2 * RANK] = (cross - high.astype(F32)).astype(BF16)
 
     arrived_if(y != holder, bb, "by")
     drain(*leaving)
@@ -541,14 +524,13 @@
             sds((NY, NC, NX, 8, 1024), BF16),
             sds((NC, 32, WIDE), BF16),
             sds((BLOCK, 256), F32),
-            sds((256, 2 * RANK), BF16),
+            sds((2, NX, NC, 16, HALF), BF16),
+            sds((NY, 2, NX, NC, 16, PART), BF16),
+            sds(base.shape, BF16),
         ),
         in_specs=[hbm, hbm, smem] + [hbm] * 8,
-        out_specs=(vmem,) * 6,
+        out_specs=(vmem,) * 8,
         scratch_shapes=[
-            pltpu.VMEM((2, NX, NC, 16, 4096), BF16),
-            pltpu.VMEM((NY, 2, NX, NC, 16, 1024), BF16),
-            pltpu.VMEM(base.shape, BF16),
             pltpu.VMEM(act.shape, BF16),
             pltpu.VMEM(cot.shape, BF16),
             pltpu.VMEM(fa.shape, F32),
@@ -600,7 +582,7 @@
             pltpu.SemaphoreType.DMA((ARRIVALS,)),
         ],
         compiler_params=pltpu.CompilerParams(
-            collective_id=0, has_side_effects=True, vmem_limit_bytes=40 * 1024 * 1024
+            collective_id=0, has_side_effects=True, vmem_limit_bytes=24 * 1024 * 1024
         ),
         cost_estimate=pl.CostEstimate(
             flops=200_000_000_000, bytes_accessed=8_000_000, transcendentals=0
@@ -622,7 +604,8 @@
     ha1,
     bb,
     part,
-    cross,
+    q1,
+    q2,
     grad,
     fa,
     ma,
@@ -641,7 +624,8 @@
     rows,
     done,
 ):
-    turned = bb[...].reshape(RANK, WIDE).astype(F32).T.astype(BF16)[0:BLOCK]
+    turned = (adapter_scale * bb[...].reshape(RANK, WIDE).astype(F32).T).astype(BF16)[0:BLOCK]
+    cross = jnp.zeros((256, RANK), F32)
     copies = []
     for yy in range(NY):
         left = ha0[yy].reshape(RANK, PART)
@@ -650,23 +634,29 @@
             first = (2 * yy + h) * PART
             here = slice(first, first + PART)
             delta = dot_nn(turned, columns)
-            rows[:, here] = (base[:, here].astype(F32) + adapter_scale * delta).astype(BF16)
+            rows[:, here] = (base[:, here].astype(F32) + delta).astype(BF16)
             one = pltpu.make_async_copy(rows.at[:, here], merged.at[:, here], done.at[2 * yy + h])
             one.start()
             copies.append(one)
+            if yy < 2:
+                asked = q1[:, :, :, :, first : first + PART]
+            else:
+                asked = q2[2 * (yy - 2) + h]
+            cross = cross + dot_nt(asked.reshape(256, PART), columns)
     ua[:, 0, :], na[:, 0, :], sa[:, 0, :] = adam_update(
         fa[:, 0, :], ma[:, 0, :], va[:, 0, :], grad[0:ROWS_A]
     )
     ub[:, 0, :], nb[:, 0, :], sb[:, 0, :] = adam_update(
         fb[:, 0, :], mb[:, 0, :], vb[:, 0, :], grad[ROWS_A:ROWS]
     )
-    twice = jnp.concatenate([turned, turned], axis=1)
-    proj[...] = (part[...] + adapter_scale * dot_nt(twice, cross[...])).astype(BF16)
+    high = cross.astype(BF16)
+    rest = (cross - high.astype(F32)).astype(BF16)
+    proj[...] = (part[...] + dot_nt(turned, high) + dot_nt(turned, rest)).astype(BF16)
     for one in copies:
         one.wait()
 
 
-def merge(base, ha0, ha1, bb, part, cross, grad, fa, ma, va, fb, mb, vb):
+def merge(base, ha0, ha1, bb, part, q1, q2, grad, fa, ma, va, fb, mb, vb):
     sds = jax.ShapeDtypeStruct
     vmem = pl.BlockSpec(memory_space=pltpu.VMEM)
     a_shape, b_shape = (ROWS_A, 1, LANES), (ROWS_B, 1, LANES)
@@ -682,12 +672,12 @@
             sds(base.shape, BF16),
             sds((BLOCK, 256), BF16),
         ),
-        in_specs=[vmem] * 13,
+        in_specs=[vmem] * 14,
         out_specs=(vmem,) * 6 + (pl.BlockSpec(memory_space=pltpu.HBM), vmem),
         scratch_shapes=[pltpu.VMEM(base.shape, BF16), pltpu.SemaphoreType.DMA((2 * NY,))],
         compiler_params=pltpu.CompilerParams(vmem_limit_bytes=16 * 1024 * 1024),
         name="merge",
-    )(base, ha0, ha1, bb, part, cross, grad, fa, ma, va, fb, mb, vb)
+    )(base, ha0, ha1, bb, part, q1, q2, grad, fa, ma, va, fb, mb, vb)
 
 
 def body(
@@ -705,7 +695,7 @@
 ):
     fa, ma, va = (v.reshape(ROWS_A, 1, LANES) for v in (input_factor, input_mean, input_square))
     fb, mb, vb = (v.reshape(ROWS_B, 1, LANES) for v in (output_factor, output_mean, output_square))
-    grad, ha0, ha1, bb, part, cross = exchange(
+    grad, ha0, ha1, bb, part, q1, q2, base = exchange(
         activations,
         cotangent,
         block_keep,
@@ -719,7 +709,7 @@
         frozen_base_rows,
     )
     ua, ub, na, nb, sa, sb, merged, projected = merge(
-        frozen_base_rows, ha0, ha1, bb, part, cross, grad, fa, ma, va, fb, mb, vb
+        base, ha0, ha1, bb, part, q1, q2, grad, fa, ma, va, fb, mb, vb
     )
     return (
         ua.reshape(1, -1),

time: 64.1 us -> 62.8 us (0.980)
  Pallas kernels: 62.6 us -> 61.3 us
    pallas_call x1, Pallas kernels: 59.5 us -> 57.5 us  [exchange(): pl.pallas_call(exchange_kernel, out_shape=(sds((ROWS, LANES), F32), sds((...]
where the time goes in v5:
time: 62.8 us; the launch traced here: 62.7 us
  Pallas kernels  61.3 us (98%)
  between operations  1.38 us (2%)
    pallas_call x1, Pallas kernels, exchange(): pl.pallas_call(exchange_kernel, out_shape=(sds((ROWS, LANES), F32), sds((...  57.5 us
    pallas_call x1, Pallas kernels, merge(): pl.pallas_call(merge_kernel, out_shape=(sds(a_shape, F32), sds(b_shape, F...  3.75 us

profile of v5, /device:TPU:1, one launch (start us, length us, event | category | flops | bytes accessed | tf_op | source)
XLA Modules:
  0.0 62.7 jit_solution(11274524248497839049)
XLA Ops:
  1.3 0.0 copy-start
  1.3 0.0 copy-start.1
  1.3 0.0 copy-start.2
  1.3 0.0 copy-start.3
  1.3 0.0 copy-start.4
  1.3 0.0 copy-start.5
  1.3 57.5 %exchange.1 = (f32[44,128]{1,0:T(8,128)S(1)}, bf16[4,2,32,1024]{3,2,1,0:T(8,128)(2,1)S(1)}, bf16[4,2,4,8,1024]{4,3,2,1,0:T(8,128)(2,1)S(1)}, bf16[2,32,256]{2,1,...) custom-call(bf16[256,2048]{1,0:T(8,128)(2,1)} %act_hbm.1, ...), custom_call_target="tpu_custom_call" | custom-call | flops 199999995904 | bytes 8000000 | tf_op jit(solution)/shard_map/exchange/pallas_call | solution.py:519
  58.9 0.0 copy-done
  58.9 0.0 copy-done.1
  58.9 0.0 copy-done.2
  58.9 0.0 copy-done.3
  58.9 0.0 copy-done.4
  58.9 0.0 copy-done.5
  58.9 3.8 %merge.1 = (f32[16,1,128]{2,1,0:T(1,128)}, f32[28,1,128]{2,1,0:T(1,128)}, f32[16,1,128]{2,1,0:T(1,128)}, f32[28,1,128]{2,1,0:T(1,128)}, f32[16,1,128]{2,1,0:T(1,...) custom-call(bf16[224,8192]{1,0:T(8,128)(2,1)S(1)} %get-tuple-element.24.base, ...), custom_call_target="tpu_custom_call" | custom-call | tf_op jit(solution)/shard_map/merge/pallas_call | solution.py:663
Async XLA Ops:
  1.3 57.6 %copy-start = (f32[1,3584]{1,0:T(1,128)S(1)}, f32[1,3584]{1,0:T(1,128)}, u32[]{:S(2)}) copy-start(f32[1,3584]{1,0:T(1,128)} %param.17) | copy-start | bytes 43012
  1.3 57.6 %copy-start.1 = (f32[1,3584]{1,0:T(1,128)S(1)}, f32[1,3584]{1,0:T(1,128)}, u32[]{:S(2)}) copy-start(f32[1,3584]{1,0:T(1,128)} %param.18) | copy-start | bytes 43012
  1.3 57.6 %copy-start.2 = (f32[1,3584]{1,0:T(1,128)S(1)}, f32[1,3584]{1,0:T(1,128)}, u32[]{:S(2)}) copy-start(f32[1,3584]{1,0:T(1,128)} %param.19) | copy-start | bytes 43012
  1.3 57.6 %copy-start.3 = (f32[1,2048]{1,0:T(1,128)S(1)}, f32[1,2048]{1,0:T(1,128)}, u32[]{:S(2)}) copy-start(f32[1,2048]{1,0:T(1,128)} %param.14) | copy-start | bytes 24580
  1.3 57.6 %copy-start.4 = (f32[1,2048]{1,0:T(1,128)S(1)}, f32[1,2048]{1,0:T(1,128)}, u32[]{:S(2)}) copy-start(f32[1,2048]{1,0:T(1,128)} %param.15) | copy-start | bytes 24580
  1.3 57.6 %copy-start.5 = (f32[1,2048]{1,0:T(1,128)S(1)}, f32[1,2048]{1,0:T(1,128)}, u32[]{:S(2)}) copy-start(f32[1,2048]{1,0:T(1,128)} %param.16) | copy-start | bytes 24580

commit v6 on v5

--- a/solution.py
+++ b/solution.py
@@ -255,7 +255,7 @@
     arrived(gb.at[c, x, 0 : NZ - 1], "gbz")
     for d in range(1, NX):
         send(gb.at[c, x], gb.at[c, x], "gbx", at(x_=xs[d]))
-    send(gb.at[c, x], gb.at[c, x], "gbc", sibling)
+    send(gb.at[c, x], gb.at[c, x], "gbc0", sibling)
 
     def spread_a(core):
         stg32[...] = ga[core].reshape(32, ROWS_A, LANES).astype(F32)
@@ -287,15 +287,15 @@
     spread_a(c)
     arrived(gb.at[c, 0 : NX - 1], "gbx")
     for d in range(1, NX):
-        send(gb.at[c, from_x[d]], gb.at[c, from_x[d]], "gbc", sibling)
+        send(gb.at[c, from_x[d]], gb.at[c, from_x[d]], f"gbc{d}", sibling)
         spread_b(c, from_x[d])
     for d in range(1, NX):
         send(q1.at[zh, x, c], q1.at[zh, x, c], "p3a", at(x_=xs[d]))
     arrived(ga.at[other], "gac")
     send(q1.at[zh, x, c], q1.at[zh, x, c], "p2a", z_pair)
     spread_a(other)
-    arrived(gb.at[other], "gbc")
     for d in range(NX):
+        arrived(gb.at[other, from_x[d]], f"gbc{d}")
         spread_b(other, from_x[d])
 
     load_act.wait()
@@ -311,7 +311,7 @@
     arrived(q2.at[y, 1 - zh, x, c], "p2b")
     for d in range(1, NX):
         send(q2.at[y, :, x, c], q2.at[y, :, x, c], "p3b", at(x_=xs[d]))
-    drain("gax", "gaz", "gac", "gbz", "gbx", "gbc", "p1a", "p1b")
+    drain("gax", "gaz", "gac", "gbz", "gbx", *(f"gbc{d}" for d in range(NX)), "p1a", "p1b")
     arrived(low.at[0 : NY - 1], "low")
     total = low[0].astype(F32)
     for yy in range(1, NY):
@@ -434,6 +434,14 @@
     arrived(q1.at[0, 0 : NX - 1, c], "p3c")
     for d in range(1, NX):
         send(q1.at[:, from_x[d], c], q1.at[:, from_x[d], c], "p5a", sibling)
+    load_base.wait()
+    arrived(q2.at[:, :, :, other], "p5b")
+    total = jnp.zeros((BLOCK, 256), F32)
+    for yy in range(NY):
+        columns = slice(HALF + yy * PART, HALF + (yy + 1) * PART)
+        total = total + dot_nt(base[:, columns], q2[yy].reshape(256, PART))
+    part_out[...] = total
+
     arrived(ea0.at[0 : NX - 1], "ex")
     for xx in range(NX):
         stga[xx * NZ : (xx + 1) * NZ] = ea0[xx].astype(F32)
@@ -477,14 +485,6 @@
     for d in range(1, NY):
         send_if(holds, bs.at[ys[d]], bb, "by", d, at(y_=ys[d]))
 
-    load_base.wait()
-    arrived(q2.at[:, :, :, other], "p5b")
-    total = jnp.zeros((BLOCK, 256), F32)
-    for yy in range(NY):
-        columns = slice(HALF + yy * PART, HALF + (yy + 1) * PART)
-        total = total + dot_nt(base[:, columns], q2[yy].reshape(256, PART))
-    part_out[...] = total
-
     arrived(q1.at[:, :, other], "p5a")
     part_out[...] = part_out[...] + dot_nt(base[:, 0:HALF], q1[...].reshape(256, HALF))
     b_sends = [("bz", d) for d in range(1, NZ)] + [("bx", d) for d in range(1, NX)]
@@ -502,7 +502,7 @@
     drain(*leaving)
 
 
-ARRIVALS, SENDS = 37, 26
+ARRIVALS, SENDS = 40, 26
 
 
 def in_hbm(array):

time: 62.8 us -> 62.8 us (level)
  no operation moved by 1% of the time
where the time goes in v6:
time: 62.8 us; the launch traced here: 62.7 us
  Pallas kernels  61.3 us (98%)
  between operations  1.38 us (2%)
    pallas_call x1, Pallas kernels, exchange(): pl.pallas_call(exchange_kernel, out_shape=(sds((ROWS, LANES), F32), sds((...  57.6 us
    pallas_call x1, Pallas kernels, merge(): pl.pallas_call(merge_kernel, out_shape=(sds(a_shape, F32), sds(b_shape, F...  3.75 us

profile of v6, /device:TPU:1, one launch (start us, length us, event | category | flops | bytes accessed | tf_op | source)
XLA Modules:
  0.0 62.7 jit_solution(7961698872287569401)
XLA Ops:
  1.3 0.0 copy-start
  1.3 0.0 copy-start.1
  1.3 0.0 copy-start.2
  1.3 0.0 copy-start.3
  1.3 0.0 copy-start.4
  1.3 0.0 copy-start.5
  1.3 57.6 %exchange.1 = (f32[44,128]{1,0:T(8,128)S(1)}, bf16[4,2,32,1024]{3,2,1,0:T(8,128)(2,1)S(1)}, bf16[4,2,4,8,1024]{4,3,2,1,0:T(8,128)(2,1)S(1)}, bf16[2,32,256]{2,1,...) custom-call(bf16[256,2048]{1,0:T(8,128)(2,1)} %act_hbm.1, ...), custom_call_target="tpu_custom_call" | custom-call | flops 199999995904 | bytes 8000000 | tf_op jit(solution)/shard_map/exchange/pallas_call | solution.py:519
  58.9 0.0 copy-done
  58.9 0.0 copy-done.1
  58.9 0.0 copy-done.2
  58.9 0.0 copy-done.3
  59.0 0.0 copy-done.4
  59.0 0.0 copy-done.5
  59.0 3.7 %merge.1 = (f32[16,1,128]{2,1,0:T(1,128)}, f32[28,1,128]{2,1,0:T(1,128)}, f32[16,1,128]{2,1,0:T(1,128)}, f32[28,1,128]{2,1,0:T(1,128)}, f32[16,1,128]{2,1,0:T(1,...) custom-call(bf16[224,8192]{1,0:T(8,128)(2,1)S(1)} %get-tuple-element.24.base, ...), custom_call_target="tpu_custom_call" | custom-call | tf_op jit(solution)/shard_map/merge/pallas_call | solution.py:663
Async XLA Ops:
  1.3 57.6 %copy-start = (f32[1,3584]{1,0:T(1,128)S(1)}, f32[1,3584]{1,0:T(1,128)}, u32[]{:S(2)}) copy-start(f32[1,3584]{1,0:T(1,128)} %param.17) | copy-start | bytes 43012
  1.3 57.6 %copy-start.1 = (f32[1,3584]{1,0:T(1,128)S(1)}, f32[1,3584]{1,0:T(1,128)}, u32[]{:S(2)}) copy-start(f32[1,3584]{1,0:T(1,128)} %param.18) | copy-start | bytes 43012
  1.3 57.6 %copy-start.2 = (f32[1,3584]{1,0:T(1,128)S(1)}, f32[1,3584]{1,0:T(1,128)}, u32[]{:S(2)}) copy-start(f32[1,3584]{1,0:T(1,128)} %param.19) | copy-start | bytes 43012
  1.3 57.6 %copy-start.3 = (f32[1,2048]{1,0:T(1,128)S(1)}, f32[1,2048]{1,0:T(1,128)}, u32[]{:S(2)}) copy-start(f32[1,2048]{1,0:T(1,128)} %param.14) | copy-start | bytes 24580
  1.3 57.6 %copy-start.4 = (f32[1,2048]{1,0:T(1,128)S(1)}, f32[1,2048]{1,0:T(1,128)}, u32[]{:S(2)}) copy-start(f32[1,2048]{1,0:T(1,128)} %param.15) | copy-start | bytes 24580
  1.3 57.6 %copy-start.5 = (f32[1,2048]{1,0:T(1,128)S(1)}, f32[1,2048]{1,0:T(1,128)}, u32[]{:S(2)}) copy-start(f32[1,2048]{1,0:T(1,128)} %param.16) | copy-start | bytes 24580
